TPU v7x, 128 devices: a whole 4x4x4 slice. The times are simulated.
128 devices in a mesh: tx: 8 (over z, core), ty: 16 (over x, y).
Axes of the slice: x: 4, y: 4, z: 4, core: 2. Of those that a mesh axis runs over, the one named last changes fastest.
Arguments:
- frames: bfloat16 [8, 48, 1, 5, 384, 384], P('tx', 'ty'), may hold values from -6 to 6
- masks: int32 [8, 48, 12, 12], P('tx', 'ty'), may hold values 0 or 1
- phases: float32 [8, 48, 1], P('tx', 'ty'), may hold values from -3.140625 to 3.140625
- slot_tile: int32 [8, 48], P('tx', 'ty'), may hold values from -1 to 31, as said below
- otf: float32 [384, 384], replicated, may hold values from 0.05 to 1
- apod: float32 [384, 384], replicated, may hold values from 0.2 to 1
Outputs:
- stitched: float32 [5120, 5120], P('ty', 'tx')
Inputs may be any that keep to these rules, and one draw needn't show every extreme that they name: `slot_tile`: in each column of devices, every tile is held in exactly one slot and is named 2 h + c for its tile row h and its tile column c within that column of devices; -1 marks an empty slot. The slots of one device never hold two tiles of the same tile row. In every draw some devices of every column hold 3 tiles.
All inputs are finite; a program needn't handle non-finite values. No bound on the sum of `masks` on one device may be relied on, other than what follows from the above.
Results may differ from a plain program's by a relative error of at most 0.0068.
Values may be sent and summed in bfloat16 or wider, within the bound.
No kernel may reach another device: no remote copies, remote signals or barrier semaphores. Data moves between devices by JAX's collectives and lax.ppermute only.
A program may use at most 128 MiB of HBM per device.

v0:
```python
import math

import jax
import jax.numpy as jnp
from jax import lax
from jax.sharding import PartitionSpec as P

STRIDE = 320
GROUP_COLS = 2


wiener = 0.1
pattern_base = (37, 101)
pattern_step = (29, -53)


def passed_along(value, axis, steps):
    count = lax.axis_size(axis)
    leading, last = (max(0, -steps), min(count, count - steps))
    return lax.ppermute(value, axis, [(source, source + steps) for source in range(leading, last)])


def in_blocks(array, dim, size):
    before, after = (array.shape[:dim], array.shape[dim + 1 :])
    return jnp.moveaxis(array.reshape(*before, size, -1, *after), dim, 0)


def cut_rows(length, count):
    unit = 8 if length >= 8 * count else 1
    return [length // unit * k // count * unit for k in range(1, count)]


def laid_out(parts, dim):
    parts = jnp.moveaxis(parts, 0, dim)
    shape = parts.shape
    return parts.reshape(*shape[:dim], shape[dim] * shape[dim + 1], *shape[dim + 2 :])


def several_exchanges(array, axis, pieces, split_dim, concat_dim):
    parts = in_blocks(array, split_dim, lax.axis_size(axis))
    split_at = max(range(1, max(2, parts.ndim - 1)), key=lambda d: parts.shape[d])
    finished = []
    for piece in jnp.split(parts, cut_rows(parts.shape[split_at], pieces), axis=split_at):
        if piece.size:
            finished.append(lax.all_to_all(piece, axis, split_axis=0, concat_axis=0, tiled=True))
    return laid_out(jnp.concatenate(finished, axis=split_at), concat_dim)


def batched(pattern, operand_a, operand_b):
    return jnp.einsum(pattern, operand_a, operand_b, preferred_element_type=jnp.float32)


def plain_dot(operand_a, operand_b):
    return jnp.dot(operand_a, operand_b, preferred_element_type=jnp.float32)


def mix_bands(pattern, operand_a, operand_b):
    return jnp.einsum(pattern, operand_a, operand_b, precision=lax.Precision.HIGHEST)


def dft_tables(length):
    places = jnp.arange(length, dtype=jnp.int32)
    product = places[:, None] * places[None, :] % length
    angles = product.astype(jnp.float32) * (2.0 * math.pi / length)
    return (jnp.cos(angles).astype(jnp.bfloat16), jnp.sin(angles).astype(jnp.bfloat16))


def pattern_shift(orient):
    return (pattern_base[0] + orient * pattern_step[0], pattern_base[1] + orient * pattern_step[1])


def filter_weights(otf, apod, phase_count):
    halfway = phase_count // 2
    rolled = []
    shift_rows, shift_cols = pattern_shift(0)
    for band_place in range(phase_count):
        band_order = band_place - halfway
        rolled.append(jnp.roll(otf, (-band_order * shift_rows, -band_order * shift_cols), (0, 1)))
    rolled_stack = jnp.stack(rolled)
    denominator = wiener + jnp.sum(rolled_stack * rolled_stack, axis=0)
    return rolled_stack * (apod / denominator)[None]


def tile_image(planes, cell_mask, offsets, gain_maps, cosine, sine_table):
    orient_count, phase_count, length = (planes.shape[0], planes.shape[1], planes.shape[2])
    cell_count = cell_mask.shape[0]
    cell_width = length // cell_count
    shaped = planes.reshape(
        orient_count * phase_count, cell_count, cell_width, cell_count, cell_width
    )
    masked = (shaped * cell_mask.astype(jnp.bfloat16)[None, :, None, :, None]).reshape(
        orient_count * phase_count, length, length
    )
    first_real = batched("pjk,kl->pjl", masked, cosine).astype(jnp.bfloat16)
    first_imag = (-batched("pjk,kl->pjl", masked, sine_table)).astype(jnp.bfloat16)
    four_real = batched("jk,pkl->pjl", cosine, first_real) + batched(
        "jk,pkl->pjl", sine_table, first_imag
    )
    four_imag = batched("jk,pkl->pjl", cosine, first_imag) - batched(
        "jk,pkl->pjl", sine_table, first_real
    )
    halfway = phase_count // 2
    orders = jnp.arange(-halfway, halfway + 1).astype(jnp.float32)
    phase_steps = jnp.arange(phase_count).astype(jnp.float32) * (2.0 * math.pi / phase_count)
    spec_real = jnp.zeros((length, length), jnp.float32)
    spec_imag = jnp.zeros((length, length), jnp.float32)
    shift_rows, shift_cols = pattern_shift(0)
    angles = orders[:, None] * (offsets[0] + phase_steps)[None, :]
    coef_real = jnp.cos(angles) / phase_count
    coef_imag = jnp.sin(angles) / phase_count
    band_real = mix_bands("mp,pxy->mxy", coef_real, four_real) + mix_bands(
        "mp,pxy->mxy", coef_imag, four_imag
    )
    band_imag = mix_bands("mp,pxy->mxy", coef_real, four_imag) - mix_bands(
        "mp,pxy->mxy", coef_imag, four_real
    )
    for band_place in range(phase_count):
        band_order = band_place - halfway
        offset_pair = (-band_order * shift_rows, -band_order * shift_cols)
        gain_map = gain_maps[band_place]
        spec_real = spec_real + gain_map * jnp.roll(band_real[band_place], offset_pair, (0, 1))
        spec_imag = spec_imag + gain_map * jnp.roll(band_imag[band_place], offset_pair, (0, 1))
    wave_real = spec_real.astype(jnp.bfloat16)
    wave_imag = spec_imag.astype(jnp.bfloat16)
    mid_real = (plain_dot(wave_real, cosine) - plain_dot(wave_imag, sine_table)).astype(
        jnp.bfloat16
    )
    mid_imag = (plain_dot(wave_real, sine_table) + plain_dot(wave_imag, cosine)).astype(
        jnp.bfloat16
    )
    return (plain_dot(cosine, mid_real) - plain_dot(sine_table, mid_imag)) * (
        1.0 / (length * length)
    )


def ramp_weights(length, intersection, is_last):
    places = jnp.arange(length).astype(jnp.float32) + 0.5
    rising = jnp.minimum(places / intersection, 1.0)
    falling = jnp.minimum((length - places) / intersection, 1.0)
    return rising * jnp.where(is_last, jnp.ones_like(falling), falling)


def blended(picture, row_last, column_last, intersection):
    length = picture.shape[0]
    weighted = (
        picture
        * ramp_weights(length, intersection, row_last)[:, None]
        * ramp_weights(length, intersection, column_last)[None, :]
    )
    return weighted.astype(jnp.bfloat16)


def fold_rows(padded_block, intersection):
    arrived = passed_along(padded_block[:intersection].astype(jnp.bfloat16), "ty", -1).astype(
        jnp.float32
    )
    interior = padded_block[intersection:]
    keep_rows = interior.shape[0] - intersection
    return jnp.concatenate([interior[:keep_rows], interior[keep_rows:] + arrived], axis=0)


def fold_columns(padded_block, intersection):
    arrived = passed_along(padded_block[:, :intersection].astype(jnp.bfloat16), "tx", -1).astype(
        jnp.float32
    )
    interior = padded_block[:, intersection:]
    keep_cols = interior.shape[1] - intersection
    return jnp.concatenate([interior[:, :keep_cols], interior[:, keep_cols:] + arrived], axis=1)


def shards(frames, masks, phases, slot_tile, otf, apod):
    row_count = lax.axis_size("ty")
    group_count = lax.axis_size("tx")
    my_group = lax.axis_index("tx")
    length = otf.shape[0]
    intersection = length - STRIDE
    cosine, sine_table = dft_tables(length)
    gain_maps = filter_weights(otf, apod, frames.shape[3])
    own_tiles = slot_tile[0]

    def one_slot(slot_items):
        planes, cell_mask, offsets, tile_id = slot_items
        picture = tile_image(planes, cell_mask, offsets, gain_maps, cosine, sine_table)
        tile_row = tile_id // GROUP_COLS
        column = GROUP_COLS * my_group + tile_id % GROUP_COLS
        result = blended(
            picture, tile_row == row_count - 1, column == GROUP_COLS * group_count - 1, intersection
        )
        return jnp.where(tile_id >= 0, result, jnp.zeros_like(result))

    results = lax.map(one_slot, (frames[0], masks[0], phases[0], own_tiles))
    column_places = jnp.arange(GROUP_COLS, dtype=jnp.int32)
    owner_rows = jnp.arange(row_count, dtype=jnp.int32)
    matches = ((own_tiles // GROUP_COLS)[:, None] == owner_rows[None, :]) & (own_tiles >= 0)[
        :, None
    ]
    choose = matches.astype(jnp.bfloat16)
    outgoing = batched("sh,sxy->hxy", choose, results).astype(jnp.bfloat16)
    labels = jnp.sum(matches.astype(jnp.int32) * (own_tiles % GROUP_COLS + 1)[:, None], axis=0) - 1
    incoming, column_tags = (
        several_exchanges(outgoing, "ty", 2, 0, 0),
        several_exchanges(labels[:, None], "ty", 2, 0, 0),
    )
    selector = (column_tags == column_places[None, :]).astype(jnp.bfloat16)
    tiles_here = batched("sc,sxy->cxy", selector, incoming)
    padded = jnp.zeros((length, STRIDE * GROUP_COLS + intersection), jnp.float32)
    for column_place in range(GROUP_COLS):
        padded = padded + jnp.pad(
            tiles_here[column_place],
            ((0, 0), (STRIDE * column_place, STRIDE * (GROUP_COLS - 1 - column_place))),
        )
    stitched = fold_columns(fold_rows(padded, intersection), intersection)
    return stitched


def solution(mesh):
    in_specs = (
        P("tx", "ty", None, None, None, None),
        P("tx", "ty", None, None),
        P("tx", "ty", None),
        P("tx", "ty"),
        P(),
        P(),
    )
    out_specs = P("ty", "tx")
    return jax.shard_map(shards, mesh=mesh, in_specs=in_specs, out_specs=out_specs, check_vma=False)
```

profile of v0, /device:TPU:1, one launch (start us, length us, event | category | flops | bytes accessed | tf_op | source)
XLA Modules:
  0.0 409.0 jit_solution(6581017391436766933)
XLA Ops:
  2.7 7.6 %all-to-all-start = ((s32[16,1,1]{2,1,0:T(1,128)}), s32[16,1,1]{2,1,0:T(1,128)}, u32[]{:S(2)}, u32[]{:S(2)}) async-start(s32[16,1,1]{2,1,0:T(1,128)} %copy.105), calls=%async_computation | async-start | bytes 16384 | tf_op jit(solution)/shard_map/all_to_all | solution.py:45
  15.6 291.3 %while.14 = (s32[]{:T(128)}, bf16[3,384,384]{1,2,0:T(8,128)(2,1)}, s32[3]{0:T(128)S(1)}, f32[5,384,384]{2,1,0:T(8,128)S(1)}, f32[3,1]{0,1:T(1,128)S(1)}, /*index...) while((s32[]{:T(128)}, bf16[3,384,384]{1,2,0:T(8,128)(2,1)}, ...), condition=%wide.region_3.4_spmd.clone.clone, body=%wide.region_2.3_spmd.clone.clone.sunk | while | flops 4285588224 | bytes 185773616 | solution.py:191
  37.0 5.8 %copy.138 = f32[5,384,384]{2,0,1:T(8,128)} copy(f32[5,384,384]{1,2,0:T(8,128)} %add_bitcast_fusion.3) | data formatting | bytes 5898240 | tf_op jit(solution)/shard_map/while/body/eval_jaxpr/add | solution.py:96
  44.1 8.8 %fusion.252 = f32[5,384,384]{2,0,1:T(8,128)} fusion(f32[5,384,384]{2,0,1:T(8,128)} %copy.138, f32[5]{0:T(128)S(1)} %multiply_add_fusion.2, f32[5]{0:T(128)S(1)} %add_convert_fusion.2), kind=kOutput, calls=%fused_computation.121.clone.1 | convolution fusion | flops 44236848 | bytes 5898280 | tf_op jit(solution)/shard_map/while/body/eval_jaxpr/mp,pxy->mxy/dot_general | solution.py:58
  60.5 5.4 %copy.137 = f32[5,384,384]{2,0,1:T(8,128)} copy(f32[5,384,384]{1,2,0:T(8,128)} %subtract_bitcast_fusion.2) | data formatting | bytes 5898240 | tf_op jit(solution)/shard_map/while/body/eval_jaxpr/sub | solution.py:99
  65.8 6.3 %fusion.253 = f32[5,384,384]{2,0,1:T(8,128)S(1)} fusion(f32[5,384,384]{2,0,1:T(8,128)} %copy.137, f32[5]{0:T(128)S(1)} %multiply_add_fusion.2, f32[5]{0:T(128)S(1)} %add_convert_fusion.2), kind=kOutput, calls=%fused_computation.117.clone.1 | convolution fusion | flops 44236848 | bytes 5898280 | tf_op jit(solution)/shard_map/while/body/eval_jaxpr/mp,pxy->mxy/dot_general | solution.py:58
  76.1 5.0 %fusion.247 = f32[5,384,384]{2,0,1:T(8,128)S(1)} fusion(f32[5,384,384]{2,0,1:T(8,128)S(1)} %bitcast.254, f32[5]{0:T(128)S(1)} %multiply_add_fusion.2, f32[5]{0:T(128)S(1)} %add_convert_fusion.2), kind=kOutput, calls=%fused_computation.118.clone.1 | convolution fusion | flops 44236848 | bytes 5898280 | tf_op jit(solution)/shard_map/while/body/eval_jaxpr/mp,pxy->mxy/dot_general | solution.py:58
  81.1 5.0 %fusion.245 = f32[5,384,384]{2,0,1:T(8,128)S(1)} fusion(f32[5,384,384]{2,0,1:T(8,128)S(1)} %bitcast.256, f32[5]{0:T(128)S(1)} %multiply_add_fusion.2, f32[5]{0:T(128)S(1)} %add_convert_fusion.2), kind=kOutput, calls=%fused_computation.122.clone.1 | convolution fusion | flops 44236848 | bytes 5898280 | tf_op jit(solution)/shard_map/while/body/eval_jaxpr/mp,pxy->mxy/dot_general | solution.py:58
  132.0 5.5 %copy.138 = f32[5,384,384]{2,0,1:T(8,128)} copy(f32[5,384,384]{1,2,0:T(8,128)} %add_bitcast_fusion.3) | data formatting | bytes 5898240 | tf_op jit(solution)/shard_map/while/body/eval_jaxpr/add | solution.py:96
  138.8 8.8 %fusion.252 = f32[5,384,384]{2,0,1:T(8,128)} fusion(f32[5,384,384]{2,0,1:T(8,128)} %copy.138, f32[5]{0:T(128)S(1)} %multiply_add_fusion.2, f32[5]{0:T(128)S(1)} %add_convert_fusion.2), kind=kOutput, calls=%fused_computation.121.clone.1 | convolution fusion | flops 44236848 | bytes 5898280 | tf_op jit(solution)/shard_map/while/body/eval_jaxpr/mp,pxy->mxy/dot_general | solution.py:58
  155.2 5.4 %copy.137 = f32[5,384,384]{2,0,1:T(8,128)} copy(f32[5,384,384]{1,2,0:T(8,128)} %subtract_bitcast_fusion.2) | data formatting | bytes 5898240 | tf_op jit(solution)/shard_map/while/body/eval_jaxpr/sub | solution.py:99
  160.5 6.6 %fusion.253 = f32[5,384,384]{2,0,1:T(8,128)S(1)} fusion(f32[5,384,384]{2,0,1:T(8,128)} %copy.137, f32[5]{0:T(128)S(1)} %multiply_add_fusion.2, f32[5]{0:T(128)S(1)} %add_convert_fusion.2), kind=kOutput, calls=%fused_computation.117.clone.1 | convolution fusion | flops 44236848 | bytes 5898280 | tf_op jit(solution)/shard_map/while/body/eval_jaxpr/mp,pxy->mxy/dot_general | solution.py:58
  171.0 5.0 %fusion.247 = f32[5,384,384]{2,0,1:T(8,128)S(1)} fusion(f32[5,384,384]{2,0,1:T(8,128)S(1)} %bitcast.254, f32[5]{0:T(128)S(1)} %multiply_add_fusion.2, f32[5]{0:T(128)S(1)} %add_convert_fusion.2), kind=kOutput, calls=%fused_computation.118.clone.1 | convolution fusion | flops 44236848 | bytes 5898280 | tf_op jit(solution)/shard_map/while/body/eval_jaxpr/mp,pxy->mxy/dot_general | solution.py:58
  176.0 5.0 %fusion.245 = f32[5,384,384]{2,0,1:T(8,128)S(1)} fusion(f32[5,384,384]{2,0,1:T(8,128)S(1)} %bitcast.256, f32[5]{0:T(128)S(1)} %multiply_add_fusion.2, f32[5]{0:T(128)S(1)} %add_convert_fusion.2), kind=kOutput, calls=%fused_computation.122.clone.1 | convolution fusion | flops 44236848 | bytes 5898280 | tf_op jit(solution)/shard_map/while/body/eval_jaxpr/mp,pxy->mxy/dot_general | solution.py:58
  226.8 5.7 %copy.138 = f32[5,384,384]{2,0,1:T(8,128)} copy(f32[5,384,384]{1,2,0:T(8,128)} %add_bitcast_fusion.3) | data formatting | bytes 5898240 | tf_op jit(solution)/shard_map/while/body/eval_jaxpr/add | solution.py:96
  233.7 8.8 %fusion.252 = f32[5,384,384]{2,0,1:T(8,128)} fusion(f32[5,384,384]{2,0,1:T(8,128)} %copy.138, f32[5]{0:T(128)S(1)} %multiply_add_fusion.2, f32[5]{0:T(128)S(1)} %add_convert_fusion.2), kind=kOutput, calls=%fused_computation.121.clone.1 | convolution fusion | flops 44236848 | bytes 5898280 | tf_op jit(solution)/shard_map/while/body/eval_jaxpr/mp,pxy->mxy/dot_general | solution.py:58
  250.1 5.4 %copy.137 = f32[5,384,384]{2,0,1:T(8,128)} copy(f32[5,384,384]{1,2,0:T(8,128)} %subtract_bitcast_fusion.2) | data formatting | bytes 5898240 | tf_op jit(solution)/shard_map/while/body/eval_jaxpr/sub | solution.py:99
  255.4 6.3 %fusion.253 = f32[5,384,384]{2,0,1:T(8,128)S(1)} fusion(f32[5,384,384]{2,0,1:T(8,128)} %copy.137, f32[5]{0:T(128)S(1)} %multiply_add_fusion.2, f32[5]{0:T(128)S(1)} %add_convert_fusion.2), kind=kOutput, calls=%fused_computation.117.clone.1 | convolution fusion | flops 44236848 | bytes 5898280 | tf_op jit(solution)/shard_map/while/body/eval_jaxpr/mp,pxy->mxy/dot_general | solution.py:58
  270.7 5.0 %fusion.245 = f32[5,384,384]{2,0,1:T(8,128)S(1)} fusion(f32[5,384,384]{2,0,1:T(8,128)S(1)} %bitcast.256, f32[5]{0:T(128)S(1)} %multiply_add_fusion.2, f32[5]{0:T(128)S(1)} %add_convert_fusion.2), kind=kOutput, calls=%fused_computation.122.clone.1 | convolution fusion | flops 44236848 | bytes 5898280 | tf_op jit(solution)/shard_map/while/body/eval_jaxpr/mp,pxy->mxy/dot_general | solution.py:58
  315.2 6.6 %all-to-all-start.1 = ((bf16[16,1,192,384]{3,2,1,0:T(8,128)(2,1)}), bf16[16,1,192,384]{3,2,1,0:T(8,128)(2,1)S(1)}, u32[]{:S(2)}, u32[]{:S(2)}) async-start(bf16[16,1,192,384]{3,2,1,0:T(8,128)(2,1)} %copy.107), calls=%async_computation.1 | async-start | bytes 4718592 | tf_op jit(solution)/shard_map/all_to_all | solution.py:45
  325.5 25.1 %all-to-all-done.1 = bf16[16,1,192,384]{3,2,1,0:T(8,128)(2,1)S(1)} async-done(((bf16[16,1,192,384]{3,2,1,0:T(8,128)(2,1)}), bf16[16,1,192,384]{3,2,1,0:T(8,128)(2,1)S(1)}, u32[]{:S(2)}, u32[]{:S(2)}) %all-to-all-start.1) | async-done | bytes 2359328 | tf_op jit(solution)/shard_map/all_to_all | solution.py:45
  350.6 5.7 %all-to-all-start.2 = ((bf16[16,1,192,384]{3,2,1,0:T(8,128)(2,1)}), bf16[16,1,192,384]{3,2,1,0:T(8,128)(2,1)}, u32[]{:S(2)}, u32[]{:S(2)}) async-start(bf16[16,1,192,384]{3,2,1,0:T(8,128)(2,1)} %copy.108), calls=%async_computation.2 | async-start | bytes 4718592 | tf_op jit(solution)/shard_map/all_to_all | solution.py:45
  360.2 23.9 %all-to-all-done.2 = bf16[16,1,192,384]{3,2,1,0:T(8,128)(2,1)} async-done(((bf16[16,1,192,384]{3,2,1,0:T(8,128)(2,1)}), bf16[16,1,192,384]{3,2,1,0:T(8,128)(2,1)}, u32[]{:S(2)}, u32[]{:S(2)}) %all-to-all-start.2) | async-done | bytes 2359328 | tf_op jit(solution)/shard_map/all_to_all | solution.py:45
  394.5 9.5 %collective-permute-start.1 = (bf16[320,64]{1,0:T(8,128)(2,1)S(1)}, bf16[320,64]{1,0:T(8,128)(2,1)S(1)}, u32[]{:S(2)}, u32[]{:S(2)}) collective-permute-start(bf16[320,64]{1,0:T(8,128)(2,1)S(1)} %fusion.151), channel_id=1, source_target_pairs={{16,0},{32,16},{48,32},{64,48},{80,64},{96,80},{112,96},{17,1},{33... | collective-permute-start | bytes 122888 | tf_op jit(solution)/shard_map/ppermute | solution.py:20
  (248 shorter events, 208.7 us)
Async XLA Ops:
  0.0 12.5 %copy-start.4 = (f32[384,384]{1,0:T(8,128)S(1)}, f32[384,384]{1,0:T(8,128)}, u32[]{:S(2)}) copy-start(f32[384,384]{1,0:T(8,128)} %param.12) | copy-start | bytes 1769476
  2.7 312.5 %all-to-all-start = ((s32[16,1,1]{2,1,0:T(1,128)}), s32[16,1,1]{2,1,0:T(1,128)}, u32[]{:S(2)}, u32[]{:S(2)}) async-start(s32[16,1,1]{2,1,0:T(1,128)} %copy.105), calls=%async_computation | async-start | bytes 16384 | tf_op jit(solution)/shard_map/all_to_all | solution.py:45
  15.6 293.8 %copy-start.10 = (s32[3]{0:T(128)S(1)}, s32[3]{0:T(128)}, u32[]{:S(2)}) copy-start(s32[3]{0:T(128)} %copy-done.9) | copy-start | bytes 40
  15.6 293.8 %copy-start.12 = (pred[3]{0:T(512)(128)(4,1)S(1)}, pred[3]{0:T(512)(128)(4,1)}, u32[]{:S(2)}) copy-start(pred[3]{0:T(512)(128)(4,1)} %copy-done.11) | copy-start | bytes 13
  24.0 7.3 %copy-start = (bf16[5,384,384]{2,1,0:T(8,128)(2,1)}, bf16[5,384,384]{2,1,0:T(8,128)(2,1)S(1)}, u32[]{:S(2)}) copy-start(bf16[5,384,384]{2,1,0:T(8,128)(2,1)S(1)} %convolution_convert_fusion.2) | copy-start | bytes 4423684 | tf_op jit(solution)/shard_map/while
  44.1 8.8 %copy-start.3 = (bf16[5,384,384]{2,1,0:T(8,128)(2,1)S(1)}, bf16[5,384,384]{2,1,0:T(8,128)(2,1)}, u32[]{:S(2)}) copy-start(bf16[5,384,384]{2,1,0:T(8,128)(2,1)} %copy-done.2) | copy-start | bytes 4423684 | tf_op jit(solution)/shard_map/while
  60.5 11.7 %slice-start.4 = ((s8[4718592]{0:T(1024)(128)(4,1)}), s8[524288]{0:T(1024)(128)(4,1)S(1)}, s32[]{:S(2)}) async-start(s8[4718592]{0:T(1024)(128)(4,1)} %bitcast.257), calls=%async_computation.7 | async-start | bytes 1048576 | tf_op jit(solution)/shard_map/while
  65.8 6.4 %slice-start.5 = ((s8[4718592]{0:T(1024)(128)(4,1)}), s8[4194304]{0:T(1024)(128)(4,1)S(1)}, s32[]{:S(2)}) async-start(s8[4718592]{0:T(1024)(128)(4,1)} %bitcast.257), calls=%async_computation.8 | async-start | bytes 8388608 | tf_op jit(solution)/shard_map/while
  74.0 7.1 %slice-start.2 = ((s8[4718592]{0:T(1024)(128)(4,1)}), s8[4194304]{0:T(1024)(128)(4,1)S(1)}, s32[]{:S(2)}) async-start(s8[4718592]{0:T(1024)(128)(4,1)} %bitcast.255), calls=%async_computation.5 | async-start | bytes 8388608 | tf_op jit(solution)/shard_map/while
  119.0 7.3 %copy-start = (bf16[5,384,384]{2,1,0:T(8,128)(2,1)}, bf16[5,384,384]{2,1,0:T(8,128)(2,1)S(1)}, u32[]{:S(2)}) copy-start(bf16[5,384,384]{2,1,0:T(8,128)(2,1)S(1)} %convolution_convert_fusion.2) | copy-start | bytes 4423684 | tf_op jit(solution)/shard_map/while
  138.8 8.8 %copy-start.3 = (bf16[5,384,384]{2,1,0:T(8,128)(2,1)S(1)}, bf16[5,384,384]{2,1,0:T(8,128)(2,1)}, u32[]{:S(2)}) copy-start(bf16[5,384,384]{2,1,0:T(8,128)(2,1)} %copy-done.2) | copy-start | bytes 4423684 | tf_op jit(solution)/shard_map/while
  155.2 11.9 %slice-start.4 = ((s8[4718592]{0:T(1024)(128)(4,1)}), s8[524288]{0:T(1024)(128)(4,1)S(1)}, s32[]{:S(2)}) async-start(s8[4718592]{0:T(1024)(128)(4,1)} %bitcast.257), calls=%async_computation.7 | async-start | bytes 1048576 | tf_op jit(solution)/shard_map/while
  160.5 6.6 %slice-start.5 = ((s8[4718592]{0:T(1024)(128)(4,1)}), s8[4194304]{0:T(1024)(128)(4,1)S(1)}, s32[]{:S(2)}) async-start(s8[4718592]{0:T(1024)(128)(4,1)} %bitcast.257), calls=%async_computation.8 | async-start | bytes 8388608 | tf_op jit(solution)/shard_map/while
  168.9 7.1 %slice-start.2 = ((s8[4718592]{0:T(1024)(128)(4,1)}), s8[4194304]{0:T(1024)(128)(4,1)S(1)}, s32[]{:S(2)}) async-start(s8[4718592]{0:T(1024)(128)(4,1)} %bitcast.255), calls=%async_computation.5 | async-start | bytes 8388608 | tf_op jit(solution)/shard_map/while
  213.7 7.3 %copy-start = (bf16[5,384,384]{2,1,0:T(8,128)(2,1)}, bf16[5,384,384]{2,1,0:T(8,128)(2,1)S(1)}, u32[]{:S(2)}) copy-start(bf16[5,384,384]{2,1,0:T(8,128)(2,1)S(1)} %convolution_convert_fusion.2) | copy-start | bytes 4423684 | tf_op jit(solution)/shard_map/while
  233.7 8.8 %copy-start.3 = (bf16[5,384,384]{2,1,0:T(8,128)(2,1)S(1)}, bf16[5,384,384]{2,1,0:T(8,128)(2,1)}, u32[]{:S(2)}) copy-start(bf16[5,384,384]{2,1,0:T(8,128)(2,1)} %copy-done.2) | copy-start | bytes 4423684 | tf_op jit(solution)/shard_map/while
  250.1 11.7 %slice-start.4 = ((s8[4718592]{0:T(1024)(128)(4,1)}), s8[524288]{0:T(1024)(128)(4,1)S(1)}, s32[]{:S(2)}) async-start(s8[4718592]{0:T(1024)(128)(4,1)} %bitcast.257), calls=%async_computation.7 | async-start | bytes 1048576 | tf_op jit(solution)/shard_map/while
  255.4 6.4 %slice-start.5 = ((s8[4718592]{0:T(1024)(128)(4,1)}), s8[4194304]{0:T(1024)(128)(4,1)S(1)}, s32[]{:S(2)}) async-start(s8[4718592]{0:T(1024)(128)(4,1)} %bitcast.257), calls=%async_computation.8 | async-start | bytes 8388608 | tf_op jit(solution)/shard_map/while
  263.6 7.1 %slice-start.2 = ((s8[4718592]{0:T(1024)(128)(4,1)}), s8[4194304]{0:T(1024)(128)(4,1)S(1)}, s32[]{:S(2)}) async-start(s8[4718592]{0:T(1024)(128)(4,1)} %bitcast.255), calls=%async_computation.5 | async-start | bytes 8388608 | tf_op jit(solution)/shard_map/while
  315.2 35.4 %all-to-all-start.1 = ((bf16[16,1,192,384]{3,2,1,0:T(8,128)(2,1)}), bf16[16,1,192,384]{3,2,1,0:T(8,128)(2,1)S(1)}, u32[]{:S(2)}, u32[]{:S(2)}) async-start(bf16[16,1,192,384]{3,2,1,0:T(8,128)(2,1)} %copy.107), calls=%async_computation.1 | async-start | bytes 4718592 | tf_op jit(solution)/shard_map/all_to_all | solution.py:45
  350.6 33.5 %all-to-all-start.2 = ((bf16[16,1,192,384]{3,2,1,0:T(8,128)(2,1)}), bf16[16,1,192,384]{3,2,1,0:T(8,128)(2,1)}, u32[]{:S(2)}, u32[]{:S(2)}) async-start(bf16[16,1,192,384]{3,2,1,0:T(8,128)(2,1)} %copy.108), calls=%async_computation.2 | async-start | bytes 4718592 | tf_op jit(solution)/shard_map/all_to_all | solution.py:45
  360.2 26.9 %copy-start.6 = (bf16[16,1,192,384]{3,0,2,1:T(8,128)(2,1)S(1)}, bf16[16,1,192,384]{3,0,2,1:T(8,128)(2,1)}, u32[]{:S(2)}) copy-start(bf16[16,1,192,384]{3,0,2,1:T(8,128)(2,1)} %copy.109) | copy-start | bytes 7077892
  389.1 5.4 %collective-permute-start = (bf16[64,704]{1,0:T(8,128)(2,1)S(1)}, bf16[64,704]{1,0:T(8,128)(2,1)S(1)}, u32[]{:S(2)}, u32[]{:S(2)}) collective-permute-start(bf16[64,704]{1,0:T(8,128)(2,1)S(1)} %fusion.148), channel_id=1, source_target_pairs={{1,0},{2,1},{3,2},{4,3},{5,4},{6,5},{7,6},{8,7},{9,8},{10,9},{11,1... | collective-permute-start | bytes 270344 | tf_op jit(solution)/shard_map/ppermute | solution.py:20
  394.5 13.2 %collective-permute-start.1 = (bf16[320,64]{1,0:T(8,128)(2,1)S(1)}, bf16[320,64]{1,0:T(8,128)(2,1)S(1)}, u32[]{:S(2)}, u32[]{:S(2)}) collective-permute-start(bf16[320,64]{1,0:T(8,128)(2,1)S(1)} %fusion.151), channel_id=1, source_target_pairs={{16,0},{32,16},{48,32},{64,48},{80,64},{96,80},{112,96},{17,1},{33... | collective-permute-start | bytes 122888 | tf_op jit(solution)/shard_map/ppermute | solution.py:20
  (24 other events, 47.0 us)
where the time goes:
time: 413 us; the launch traced here: 409 us
  matrix products  201 us (49%)
  local copies, waits for them, and re-layouts  81.2 us (20%)
  waiting for transfers between devices  56.2 us (14%)
  starting transfers between devices  30.8 us (7%)
  other arithmetic  21.5 us (5%)
  loops' own time  17.7 us (4%)
    dot_general x12, matrix products, mix_bands(): jnp.einsum(pattern, operand_a, operand_b, precision=lax.Precision.HIGHEST)  75.4 us
    dot_general x20, matrix products, batched(): jnp.einsum(pattern, operand_a, operand_b, preferred_element_type=jnp.floa...  74 us
    dot_general x12, matrix products, plain_dot(): return jnp.dot(operand_a, operand_b, preferred_element_type=jnp.float32)  51.6 us
    all_to_all x3, waiting for transfers between devices, several_exchanges(): lax.all_to_all(piece, axis, split_axis=0, concat_axis=0, tiled=True)  49 us
    all_to_all x3, starting transfers between devices, several_exchanges(): lax.all_to_all(piece, axis, split_axis=0, concat_axis=0, tiled=True)  19.9 us
    another operation x1, loops' own time, shards(): results = lax.map(one_slot, (frames[0], masks[0], phases[0], own_tiles))  17.7 us
    add x3, local copies, waits for them, and re-layouts, tile_image(): batched('jk,pkl->pjl', cosine, first_real)  17 us
    sub x3, local copies, waits for them, and re-layouts, tile_image(): batched('jk,pkl->pjl', cosine, first_imag)  16.1 us
  transfers between devices with their start and end apart: 5, of which 4 were waited for; matrix products, arithmetic and copies ran while one was open for 69% of the time, Pallas kernels for 0%

commit v1 on v0

v1 whole, which is shorter than its diff:
```python
import functools
import math

import jax
import jax.numpy as jnp
import numpy as np
from jax import lax
from jax.experimental import pallas as pl
from jax.experimental.pallas import tpu as pltpu
from jax.sharding import PartitionSpec as P

SIDE = 384
STRIDE = 320
OVERLAP = SIDE - STRIDE
GROUP_COLS = 2
PHASES = 5
WIENER = 0.1
SHIFT_ROWS, SHIFT_COLS = 37, 101
CHUNK = SIDE // 16
GROUP = 8

COL_A = np.arange(64, 128)
COL_B = np.arange(128, 192)
COL_C = np.arange(0, 64)
NYQUIST = SIDE // 2


def cos_sin(rows, cols):
    angle = (np.outer(rows, cols) % SIDE) * (2.0 * math.pi / SIDE)
    return np.cos(angle), np.sin(angle)


def first_table(order):
    n = np.arange(SIDE)

    def plus(cols):
        c, s = cos_sin(n, cols + order * SHIFT_COLS)
        return np.concatenate([c, -s]), np.concatenate([-s, -c])

    def minus(cols):
        c, s = cos_sin(n, cols - order * SHIFT_COLS)
        return np.concatenate([c, s]), np.concatenate([-s, c])

    blocks = [
        plus(COL_A), minus(COL_B), plus(COL_B), minus(COL_A),
        plus(COL_C), plus(np.array([NYQUIST])), minus(COL_C[1:]),
    ]
    return np.concatenate([b[0] for b in blocks] + [b[1] for b in blocks], axis=1)


def centre_table():
    n = np.arange(SIDE)
    cols = np.concatenate([COL_A, COL_B, COL_C, [NYQUIST]])
    c, s = cos_sin(n, cols)
    pad = np.zeros((SIDE, 63))
    return np.concatenate([c, pad, -s, pad], axis=1)


def forward_rows():
    c, s = cos_sin(np.arange(SIDE), np.arange(SIDE))
    return np.block([[c, s], [-s, c]])


def inverse_rows():
    c, s = cos_sin(np.arange(SIDE), np.arange(SIDE))
    return np.block([[c, -s], [s, c]])


def last_table():
    lines = np.concatenate([COL_A, COL_B, COL_C, [NYQUIST], COL_C[1:]])
    c, s = cos_sin(lines, np.arange(SIDE))
    return np.concatenate([c, -s], axis=0)


def table(values):
    return jnp.asarray(values.astype(np.float32)).astype(jnp.bfloat16)


def negated(array):
    return jnp.roll(array[::-1, ::-1], (1, 1), (0, 1))


def band_gains(otf, apod):
    halfway = PHASES // 2

    def weights(base, sign):
        moved = [
            jnp.roll(base, (-sign * m * SHIFT_ROWS, -sign * m * SHIFT_COLS), (0, 1))
            for m in range(-halfway, halfway + 1)
        ]
        total = WIENER + sum(one * one for one in moved)
        return moved, total

    moved, total = weights(otf, 1)
    back, back_total = weights(negated(otf), -1)
    scale = apod / total
    back_scale = negated(apod) / back_total

    gains = {}
    for m in range(-halfway, halfway + 1):
        gains[m] = moved[m + halfway] * scale + back[halfway - m] * back_scale

    tiles = []
    for m in (1, 2):
        up, down = gains[m], gains[-m]
        tiles += [
            up[:, 64:128], down[:, 128:192],
            up[:, 128:192], down[:, 64:128],
            up[:, 0:64], up[:, 192:193], down[:, 1:64],
        ]
    mid = gains[0]
    zeros = jnp.zeros((SIDE, 63), jnp.float32)
    tiles += [mid[:, 64:192], 0.5 * mid[:, 0:1], mid[:, 1:64], 0.5 * mid[:, 192:193], zeros]
    return jnp.concatenate(tiles, axis=1)


def tile_kernel(
    last_ref, frames_ref, masks_ref, turn_ref, gains_ref, rows_ref, cols_ref,
    w1_ref, w2_ref, w0_ref, fwd_ref, inv_ref, out_w_ref, out_ref, left_ref, y_ref, t_ref, s_ref,
):
    slot = pl.program_id(0)
    f32, bf16 = jnp.float32, jnp.bfloat16
    c1, c2 = math.cos(2 * math.pi / 5), math.cos(4 * math.pi / 5)
    n1, n2 = math.sin(2 * math.pi / 5), math.sin(4 * math.pi / 5)

    for cell in range(12):
        rows = pl.ds(32 * cell, 32)
        flag = masks_ref[0, cell : cell + 1, :]
        f = [frames_ref[0, p, rows, :].astype(f32) * flag for p in range(PHASES)]
        s1, d1, s2, d2 = f[1] + f[4], f[1] - f[4], f[2] + f[3], f[2] - f[3]
        left_ref[rows, 1536:1920] = ((f[0] + s1 + s2) * (1.0 / PHASES)).astype(bf16)
        for at, (a, b) in enumerate((
            (f[0] + c1 * s1 + c2 * s2, n1 * d1 + n2 * d2),
            (f[0] + c2 * s1 + c1 * s2, n2 * d1 - n1 * d2),
        )):
            c = turn_ref[0, rows, 2 * at : 2 * at + 1]
            s = turn_ref[0, rows, 2 * at + 1 : 2 * at + 2]
            left_ref[rows, 768 * at : 768 * at + 384] = (c * a - s * b).astype(bf16)
            left_ref[rows, 768 * at + 384 : 768 * at + 768] = (c * b + s * a).astype(bf16)

    def dot(x, w):
        return jnp.dot(x, w, preferred_element_type=f32)

    for at, w_ref in enumerate((w1_ref, w2_ref)):
        for part in range(3):
            lanes = pl.ds(256 * part, 256)
            r = dot(left_ref[:, 768 * at : 768 * at + 768], w_ref[:, lanes]).astype(bf16)
            for half in range(2):
                tile = 2 * part + half
                base = 384 if tile >= 3 else 0
                col = 384 * at + 128 * (tile % 3)
                y_ref[base : base + 384, col : col + 128] = r[:, 128 * half : 128 * half + 128]
    for part in range(2):
        r = dot(left_ref[:, 1536:1920], w0_ref[:, 256 * part : 256 * part + 256]).astype(bf16)
        y_ref[384 * part : 384 * part + 384, 768:1024] = r

    for half in range(2):
        rows = pl.ds(384 * half, 384)
        lhs = fwd_ref[rows, :]

        def part(n):
            return dot(lhs, y_ref[:, 256 * n : 256 * n + 256]) * gains_ref[:, 256 * n : 256 * n + 256]

        d = part(0)
        t_ref[:, 0:256] = d
        d = part(1)
        t_ref[:, 256:384] = d[:, 0:128]
        t_ref[:, 0:128] += d[:, 128:256]
        d = part(2)
        t_ref[:, 128:384] += d
        d = part(3)
        s_ref[rows, 0:128] = (t_ref[:, 0:128] + pltpu.roll(t_ref[:, 128:256], 64, 1) + d[:, 0:128]).astype(bf16)
        s_ref[rows, 128:256] = (t_ref[:, 256:384] + d[:, 128:256]).astype(bf16)

    mid_real = dot(inv_ref[0:384, :], s_ref[...]).astype(bf16)
    mid_imag = dot(inv_ref[384:768, :], s_ref[...]).astype(bf16)
    picture = dot(mid_real, out_w_ref[0:256, :]) + dot(mid_imag, out_w_ref[256:512, :])
    row_last = last_ref[slot, 0]
    col_last = last_ref[slot, 1]
    row_ramp = rows_ref[:, 0:1] * jnp.where(row_last > 0, 1.0, rows_ref[:, 1:2])
    col_ramp = cols_ref[0:1, :] * jnp.where(col_last > 0, 1.0, cols_ref[1:2, :])
    weighted = picture * row_ramp * col_ramp
    for chunk in range(16):
        out_ref[chunk, 0] = weighted[CHUNK * chunk : CHUNK * chunk + CHUNK, :].astype(bf16)


def ramps():
    places = np.arange(SIDE) + 0.5
    rising = np.minimum(places / OVERLAP, 1.0)
    falling = np.minimum((SIDE - places) / OVERLAP, 1.0)
    return rising, falling


def tile_results(frames, masks, phases, last, gains):
    slots = frames.shape[0]
    f32 = jnp.float32
    spread = jnp.repeat(masks.astype(f32), SIDE // masks.shape[2], axis=2)
    orders = np.arange(1, 3)
    angle = (np.outer(np.arange(SIDE), orders * SHIFT_ROWS) % SIDE) * (2 * math.pi / SIDE)
    row_c = jnp.asarray(np.cos(angle) / PHASES, f32)[None]
    row_s = jnp.asarray(np.sin(angle) / PHASES, f32)[None]
    turn = phases * jnp.asarray(orders, f32)[None]
    c, s = jnp.cos(turn)[:, None], jnp.sin(turn)[:, None]
    turns = jnp.stack([c * row_c - s * row_s, s * row_c + c * row_s], axis=3).reshape(slots, SIDE, 4)
    rising, falling = ramps()
    rows = jnp.asarray(np.stack([rising / (SIDE * SIDE), falling], axis=1), f32)
    cols = jnp.asarray(np.stack([rising, falling]), f32)
    tables = [
        table(first_table(1)), table(first_table(2)),
        table(centre_table()),
        table(forward_rows()), table(inverse_rows()), table(last_table()),
    ]

    def whole(array):
        return pl.BlockSpec(array.shape, lambda i, *_: (0,) * array.ndim)

    fixed = [gains, rows, cols] + tables
    return pl.pallas_call(
        tile_kernel,
        out_shape=jax.ShapeDtypeStruct((16, slots, CHUNK, SIDE), jnp.bfloat16),
        grid_spec=pltpu.PrefetchScalarGridSpec(
            num_scalar_prefetch=1,
            grid=(slots,),
            in_specs=[
                pl.BlockSpec((1, PHASES, SIDE, SIDE), lambda i, *_: (i, 0, 0, 0)),
                pl.BlockSpec((1, 12, SIDE), lambda i, *_: (i, 0, 0)),
                pl.BlockSpec((1, SIDE, 4), lambda i, *_: (i, 0, 0)),
            ] + [whole(one) for one in fixed],
            out_specs=pl.BlockSpec((16, 1, CHUNK, SIDE), lambda i, *_: (0, i, 0, 0)),
            scratch_shapes=[
                pltpu.VMEM((SIDE, 1920), jnp.bfloat16),
                pltpu.VMEM((2 * SIDE, 1024), jnp.bfloat16),
                pltpu.VMEM((SIDE, 384), jnp.float32),
                pltpu.VMEM((2 * SIDE, 256), jnp.bfloat16),
            ],
        ),
        cost_estimate=pl.CostEstimate(flops=slots * 3_000_000_000, bytes_accessed=12_000_000, transcendentals=0),
        name="tiles",
    )(last, frames, spread, turns, *fixed)


def pick_kernel(index_ref, in_ref, out_ref):
    def one(at, carry):
        source = index_ref[at]
        value = in_ref[jnp.maximum(source, 0)]
        out_ref[at] = jnp.where(source >= 0, value, jnp.zeros_like(value))
        return carry

    lax.fori_loop(0, out_ref.shape[0], one, 0, unroll=8)


def picked(groups, index):
    count = index.shape[0]
    return pl.pallas_call(
        pick_kernel,
        out_shape=jax.ShapeDtypeStruct((count,) + groups.shape[1:], groups.dtype),
        grid_spec=pltpu.PrefetchScalarGridSpec(
            num_scalar_prefetch=1,
            grid=(1,),
            in_specs=[pl.BlockSpec(groups.shape, lambda i, *_: (0, 0, 0))],
            out_specs=pl.BlockSpec((count,) + groups.shape[1:], lambda i, *_: (0, 0, 0)),
        ),
        name="pick",
    )(index, groups)


def shards(frames, masks, phases, slot_tile, otf, apod):
    devices = lax.axis_size("ty")
    group_count = lax.axis_size("tx")
    my_group = lax.axis_index("tx")
    me = lax.axis_index("ty")
    own = slot_tile[0]
    slots = own.shape[0]
    column = GROUP_COLS * my_group + own % GROUP_COLS
    last = jnp.stack(
        [own // GROUP_COLS == devices - 1, column == GROUP_COLS * group_count - 1], axis=1
    ).astype(jnp.int32)
    names = lax.all_to_all(jnp.broadcast_to(own[None], (devices, slots)), "ty", 0, 0, tiled=True)

    gains = band_gains(otf, apod)
    results = tile_results(frames[0, :, 0], masks[0], phases[0], last, gains)
    spread = lax.all_to_all(results, "ty", 0, 0, tiled=True)

    i = jnp.arange(CHUNK // GROUP, dtype=jnp.int32)
    ahead = ((CHUNK // GROUP) * me + i < OVERLAP // GROUP).astype(jnp.int32)
    rows = jnp.arange(devices, dtype=jnp.int32)[:, None, None] + ahead[None, None, :]
    wanted = GROUP_COLS * rows + jnp.arange(GROUP_COLS, dtype=jnp.int32)[None, :, None]
    flat = names.reshape(-1)
    hit = wanted[..., None] == flat
    place = jnp.sum(hit * jnp.arange(flat.shape[0], dtype=jnp.int32), axis=-1)
    index = jnp.where(rows < devices, place * (CHUNK // GROUP) + i, -1).reshape(-1)

    chosen = picked(spread.reshape(-1, GROUP, SIDE), index)
    home = lax.all_to_all(chosen.reshape(devices, GROUP_COLS * CHUNK, SIDE), "ty", 0, 0, tiled=True)

    tiles = home.reshape(devices, GROUP_COLS, CHUNK, SIDE).swapaxes(0, 1).reshape(GROUP_COLS, SIDE, SIDE)
    tiles = tiles.astype(jnp.float32)
    body = tiles[:, OVERLAP:]
    folded = jnp.concatenate(
        [body[:, : STRIDE - OVERLAP], body[:, STRIDE - OVERLAP :] + tiles[:, :OVERLAP]], axis=1
    )
    left, right = folded[0], folded[1]
    strip = lax.ppermute(
        left[:, :OVERLAP].astype(jnp.bfloat16), "tx", [(g, g - 1) for g in range(1, group_count)]
    ).astype(jnp.float32)
    joined = left[:, STRIDE:] + right[:, :OVERLAP]
    edge = right[:, STRIDE:] + strip
    return jnp.concatenate([left[:, OVERLAP:STRIDE], joined, right[:, OVERLAP:STRIDE], edge], axis=1)


def solution(mesh):
    in_specs = (
        P("tx", "ty", None, None, None, None),
        P("tx", "ty", None, None),
        P("tx", "ty", None),
        P("tx", "ty"),
        P(),
        P(),
    )
    return jax.shard_map(
        shards, mesh=mesh, in_specs=in_specs, out_specs=P("ty", "tx"), check_vma=False
    )
```

time: 413 us -> 108 us (0.26)
  matrix products: 201 us -> 0 us
  local copies, waits for them, and re-layouts: 81.2 us -> 28.1 us
  waiting for transfers between devices: 56.2 us -> 14.5 us
  Pallas kernels: 0 us -> 19.6 us
  loops' own time: 17.7 us -> 0 us
  blocking collectives: 0 us -> 13.5 us
  starting transfers between devices: 30.8 us -> 19.7 us
  other arithmetic: 21.5 us -> 10.8 us
    dot_general x44 -> x0, matrix products: 201 us -> none  [the longest x12 75.4 us: mix_bands(): jnp.einsum(pattern, operand_a, operand_b, precision=lax.Precision.HIGHEST)]
    all_to_all x3 -> x2, waiting for transfers between devices: 49 us -> 11.2 us  [the longest x1 11.2 us: shards(): spread = lax.all_to_all(results, 'ty', 0, 0, tiled=True)]
    pallas_call x0 -> x2, Pallas kernels: none -> 19.6 us  [the longest x1 16.6 us: tile_results(): pl.pallas_call(tile_kernel, out_shape=jax.ShapeDtypeStruct((16, slots, CH...]
    another operation x1 -> x0, loops' own time: 17.7 us -> none  [shards(): results = lax.map(one_slot, (frames[0], masks[0], phases[0], own_tiles))]
    add x3 -> x0, local copies, waits for them, and re-layouts: 17 us -> none  [tile_image(): batched('jk,pkl->pjl', cosine, first_real)]
    sub x4 -> x0, local copies, waits for them, and re-layouts: 16.8 us -> none  [the longest x3 16.1 us: tile_image(): batched('jk,pkl->pjl', cosine, first_imag)]
    all_to_all x0 -> x1, blocking collectives: none -> 13.5 us  [shards(): lax.all_to_all(chosen.reshape(devices, GROUP_COLS * CHUNK, SIDE), 'ty', 0...]
    while x67 -> x0, local copies, waits for them, and re-layouts: 12.4 us -> none
  transfers between devices with their start and end apart: 5 -> 3, of which waited for: 4 -> 2; matrix products, arithmetic and copies ran while one was open for 69% -> 31% of each run, Pallas kernels for 0% -> 16%
where the time goes in v1:
time: 108 us; the launch traced here: 107 us
  local copies, waits for them, and re-layouts  28.1 us (26%)
  starting transfers between devices  19.7 us (18%)
  Pallas kernels  19.6 us (18%)
  waiting for transfers between devices  14.5 us (13%)
  blocking collectives  13.5 us (12%)
  other arithmetic  10.8 us (10%)
    pallas_call x1, Pallas kernels, tile_results(): pl.pallas_call(tile_kernel, out_shape=jax.ShapeDtypeStruct((16, slots, CH...  16.6 us
    all_to_all x1, blocking collectives, shards(): lax.all_to_all(chosen.reshape(devices, GROUP_COLS * CHUNK, SIDE), 'ty', 0...  13.5 us
    all_to_all x1, waiting for transfers between devices, shards(): spread = lax.all_to_all(results, 'ty', 0, 0, tiled=True)  11.2 us
    slice x10, local copies, waits for them, and re-layouts, negated(): return jnp.roll(array[::-1, ::-1], (1, 1), (0, 1))  10.9 us
    all_to_all x1, starting transfers between devices, shards(): lax.all_to_all(jnp.broadcast_to(own[None], (devices, slots)), 'ty', 0, 0,...  7.57 us
    all_to_all x1, starting transfers between devices, shards(): spread = lax.all_to_all(results, 'ty', 0, 0, tiled=True)  6.67 us
    ppermute x1, starting transfers between devices, shards(): lax.ppermute(left[:, :OVERLAP].astype(jnp.bfloat16), 'tx', [(g, g - 1) fo...  5.42 us
    slice x8, local copies, waits for them, and re-layouts, weights(): jnp.roll(base, (-sign * m * SHIFT_ROWS, -sign * m * SHIFT_COLS), (0, 1))  4.63 us
  transfers between devices with their start and end apart: 3, of which 2 were waited for; matrix products, arithmetic and copies ran while one was open for 31% of the time, Pallas kernels for 16%

profile of v1, /device:TPU:1, one launch (start us, length us, event | category | flops | bytes accessed | tf_op | source)
XLA Modules:
  0.0 106.6 jit_solution(13050926962705816152)
XLA Ops:
  0.0 1.3 %broadcast_in_dim.15 = s32[16,1,3]{2,1,0:T(1,128)} broadcast(s32[3]{0:T(128)} %bitcast.26), dimensions={2} | broadcast | bytes 204 | tf_op jit(solution)/shard_map/broadcast_in_dim | solution.py:278
  1.3 7.6 %all-to-all-start = ((s32[16,1,3]{2,1,0:T(1,128)}), s32[16,1,3]{2,1,0:T(1,128)S(1)}, u32[]{:S(2)}, u32[]{:S(2)}) async-start(s32[16,1,3]{2,1,0:T(1,128)} %broadcast_in_dim.15), calls=%async_computation | async-start | bytes 16384 | tf_op jit(solution)/shard_map/all_to_all | solution.py:278
  8.8 1.2 %slice.261 = f32[383,384]{1,0:T(8,128)S(1)} slice(f32[384,384]{1,0:T(8,128)} %param.21), slice={[1:384], [0:384]} | slice | bytes 1176576 | tf_op jit(solution)/shard_map/jit(_roll_static)/slice | solution.py:80
  10.0 1.5 %slice.262 = f32[383,384]{1,0:T(8,128)S(1)} reverse(f32[383,384]{1,0:T(8,128)S(1)} %slice.261), dimensions={0,1} | reverse | bytes 1176576 | tf_op jit(solution)/shard_map/jit(_roll_static)/slice | solution.py:80
  12.7 0.9 fusion.31
  14.2 0.9 fusion.36
  15.8 0.8 fusion.34
  17.3 0.9 slice.271
  18.2 5.8 %slice.272 = f32[383,384]{1,0:T(8,128)} reverse(f32[383,384]{1,0:T(8,128)} %slice.271), dimensions={0,1} | reverse | bytes 1176576 | tf_op jit(solution)/shard_map/jit(_roll_static)/slice | solution.py:80
  24.0 1.2 %slice.270 = f32[1,384]{1,0:T(1,128)} reverse(f32[1,384]{1,0:T(1,128)S(1)} %slice-done.1), dimensions={0,1} | reverse | bytes 3072 | tf_op jit(solution)/shard_map/jit(_roll_static)/slice | solution.py:80
  25.2 1.2 %slice_maximum_fusion = (f32[384,283]{1,0:T(8,128)S(1)}, f32[384,283]{1,0:T(8,128)S(1)}) fusion(f32[37,384]{1,0:T(8,128)S(1)} %get-tuple-element.32, f32[347,384]{1,0:T(8,128)S(1)} %get-tuple-element.30, f32[37,384]{1,0:T(8,128)} %get-tuple-element.39, f32[347,384]{1,0:T(8,128)S(1)} %get-tuple-element.41), kind=kLoop, calls=%fused_computation.16 | loop fusion | flops 217344 | bytes 2049024 | tf_op jit(solution)/shard_map/jit(_roll_static)/concatenate | solution.py:88
  28.5 3.4 %multiply_add_fusion = (f32[384,384]{1,0:T(8,128)S(1)}, f32[384,384]{1,0:T(8,128)S(1)}, f32[384,384]{1,0:T(8,128)S(1)}) fusion(f32[384,384]{1,0:T(8,128)S(1)} %copy-done, f32[384,384]{1,0:T(8,128)S(1)} %copy-done.8, f32[74,384]{1,0:T(8,128)S(1)} %copy-done.10, f32[310,384]{1,0:T(8,128)S(1)} %copy-done.1, f32[384,182]{1,0:T(8,128)S(1)} %get-tuple-element.55, ...), kind=kLoop, calls=%fused_computation.38 | loop fusion | flops 7225344 | bytes 10896384 | tf_op jit(solution)/shard_map/add | solution.py:101
  34.1 0.8 slice_multiply_fusion
  35.4 1.1 %copy.40.turn_ref = f32[3,384,4]{2,1,0:T(8,128)} copy(f32[3,384,4]{1,2,0:T(4,128)S(1)} %reshape.269) | data formatting | bytes 36864 | tf_op jit(solution)/shard_map/reshape | solution.py:204
  38.2 3.4 %concatenate.99.gains_ref = f32[384,1024]{1,0:T(8,128)} concatenate(f32[384,64]{1,0:T(8,128)S(1)} %get-tuple-element.23, f32[384,64]{1,0:T(8,128)S(1)} %get-tuple-element.25, f32[384,64]{1,0:T(8,128)S(1)} %get-tuple-element.22, f32[384,64]{1,0:T(8,128)S(1)} %get-tuple-element.24, f32[384,64]{1,0:T(8,128)S(1)} %get-tuple-element.21, f32[384,1]{1,0:T(8,128)S(1)} %slice.341, ...), dimensions={1} | concatenate | bytes 3145728 | tf_op jit(solution)/shard_map/concatenate | solution.py:114
  41.6 16.6 %tiles.1 = bf16[16,3,24,384]{3,2,1,0:T(8,128)(2,1)} custom-call(s32[3,2]{1,0:T(4,128)} %add_convert_fusion.last_ref, bf16[3,5,384,384]{3,2,1,0:T(8,128)(2,1)} %bitcast.29, f32[3,12,384]{2,1,0:T(8,128)} %reshape.268.masks_ref, f32[3,384,4]{2,1,0:T(8,128)} %copy.40.turn_ref, f32[384,1024]{1,0:T(8,128)} %concatenate.99.gains_ref, ...), custom_call_target="tpu_custom_call" | custom-call | flops 8999999488 | bytes 12000000 | tf_op jit(solution)/shard_map/tiles/pallas_call | solution.py:218
  58.3 6.7 %all-to-all-start.1 = ((bf16[16,3,24,384]{3,2,1,0:T(8,128)(2,1)}), bf16[16,3,24,384]{3,2,1,0:T(8,128)(2,1)S(1)}, u32[]{:S(2)}, u32[]{:S(2)}) async-start(bf16[16,3,24,384]{3,2,1,0:T(8,128)(2,1)} %tiles.1), calls=%async_computation.1 | async-start | bytes 1769472 | tf_op jit(solution)/shard_map/all_to_all | solution.py:282
  67.4 11.2 %all-to-all-done.1 = bf16[16,3,24,384]{3,2,1,0:T(8,128)(2,1)S(1)} async-done(((bf16[16,3,24,384]{3,2,1,0:T(8,128)(2,1)}), bf16[16,3,24,384]{3,2,1,0:T(8,128)(2,1)S(1)}, u32[]{:S(2)}, u32[]{:S(2)}) %all-to-all-start.1) | async-done | bytes 884768 | tf_op jit(solution)/shard_map/all_to_all | solution.py:282
  78.6 0.9 copy-done.6
  79.5 3.0 %pick.1 = bf16[96,8,384]{2,1,0:T(8,128)(2,1)} custom-call(s32[96]{0:T(128)} %select_n.35.index_ref, bf16[144,8,384]{2,1,0:T(8,128)(2,1)} %bitcast.22), custom_call_target="tpu_custom_call" | custom-call | tf_op jit(solution)/shard_map/pick/pallas_call | solution.py:254
  82.5 13.5 %all_to_all.16 = bf16[16,48,384]{2,1,0:T(8,128)(2,1)S(1)} all-to-all(bf16[16,48,384]{2,1,0:T(8,128)(2,1)} %bitcast.24), channel_id=1, replica_groups=mesh['tx'=8,'ty'=16] {'ty'}, dimensions={0} | all-to-all | bytes 1179648 | tf_op jit(solution)/shard_map/all_to_all | solution.py:294
  96.3 5.4 %collective-permute-start = (bf16[320,64]{1,0:T(8,128)(2,1)S(1)}, bf16[320,64]{1,0:T(8,128)(2,1)S(1)}, u32[]{:S(2)}, u32[]{:S(2)}) collective-permute-start(bf16[320,64]{1,0:T(8,128)(2,1)S(1)} %slice.409), channel_id=1, source_target_pairs={{16,0},{32,16},{48,32},{64,48},{80,64},{96,80},{112,96},{17,1},{33... | collective-permute-start | bytes 122888 | tf_op jit(solution)/shard_map/ppermute | solution.py:303
  102.0 3.3 %collective-permute-done = bf16[320,64]{1,0:T(8,128)(2,1)S(1)} collective-permute-done((bf16[320,64]{1,0:T(8,128)(2,1)S(1)}, bf16[320,64]{1,0:T(8,128)(2,1)S(1)}, u32[]{:S(2)}, u32[]{:S(2)}) %collective-permute-start) | collective-permute-done | bytes 40992 | tf_op jit(solution)/shard_map/ppermute | solution.py:303
  105.5 1.1 %pad_maximum_fusion = f32[320,640]{1,0:T(8,128)} fusion(f32[320,64]{1,0:T(8,128)S(1)} %get-tuple-element.43, f32[320,256]{1,0:T(8,128)S(1)} %slice.362, f32[320,64]{1,0:T(8,128)S(1)} %get-tuple-element.42, f32[320,256]{1,0:T(8,128)S(1)} %slice.359), kind=kLoop, calls=%fused_computation.2 | loop fusion | flops 614400 | bytes 1638400 | tf_op jit(solution)/shard_map/concatenate | solution.py:308
  (98 shorter events, 12.5 us)
Async XLA Ops:
  1.3 57.0 %all-to-all-start = ((s32[16,1,3]{2,1,0:T(1,128)}), s32[16,1,3]{2,1,0:T(1,128)S(1)}, u32[]{:S(2)}, u32[]{:S(2)}) async-start(s32[16,1,3]{2,1,0:T(1,128)} %broadcast_in_dim.15), calls=%async_computation | async-start | bytes 16384 | tf_op jit(solution)/shard_map/all_to_all | solution.py:278
  8.8 2.7 %slice-start = ((f32[384,384]{1,0:T(8,128)}), f32[1,384]{1,0:T(1,128)S(1)}, s32[]{:S(2)}) async-start(f32[384,384]{1,0:T(8,128)} %param.21), calls=%async_computation.3 | async-start | bytes 3072 | tf_op jit(solution)/shard_map/jit(_roll_static)/slice | solution.py:80
  12.7 1.5 %copy-start = (f32[384,384]{1,0:T(8,128)S(1)}, f32[384,384]{1,0:T(8,128)}, u32[]{:S(2)}) copy-start(f32[384,384]{1,0:T(8,128)} %param.21) | copy-start | bytes 1769476
  15.8 1.5 %copy-start.7 = (f32[384,384]{1,0:T(8,128)S(1)}, f32[384,384]{1,0:T(8,128)}, u32[]{:S(2)}) copy-start(f32[384,384]{1,0:T(8,128)} %param.22) | copy-start | bytes 1769476
  17.3 6.7 %slice-start.1 = ((f32[384,384]{1,0:T(8,128)}), f32[1,384]{1,0:T(1,128)S(1)}, s32[]{:S(2)}) async-start(f32[384,384]{1,0:T(8,128)} %param.22), calls=%async_computation.4 | async-start | bytes 3072 | tf_op jit(solution)/shard_map/jit(_roll_static)/slice | solution.py:80
  26.5 1.0 copy-start.1
  26.5 1.0 copy-start.10
  26.5 1.3 %copy-start.8 = (f32[384,384]{1,0:T(8,128)S(1)}, f32[384,384]{1,0:T(8,128)}, u32[]{:S(2)}) copy-start(f32[384,384]{1,0:T(8,128)} %param.22) | copy-start | bytes 1769476
  26.5 1.4 %copy-start.9 = (f32[383,384]{1,0:T(8,128)S(1)}, f32[383,384]{1,0:T(8,128)}, u32[]{:S(2)}) copy-start(f32[383,384]{1,0:T(8,128)} %slice.272) | copy-start | bytes 1764868
  26.8 1.4 %copy-start.3 = (f32[383,384]{1,0:T(8,128)S(1)}, f32[383,384]{1,0:T(8,128)}, u32[]{:S(2)}) copy-start(f32[383,384]{1,0:T(8,128)} %copy-done.2) | copy-start | bytes 1764868
  26.8 1.5 %copy-start.4 = (f32[347,384]{1,0:T(8,128)S(1)}, f32[347,384]{1,0:T(8,128)}, u32[]{:S(2)}) copy-start(f32[347,384]{1,0:T(8,128)} %get-tuple-element.31) | copy-start | bytes 1598980
  26.8 1.7 %copy-start.5 = (f32[347,384]{1,0:T(8,128)S(1)}, f32[347,384]{1,0:T(8,128)}, u32[]{:S(2)}) copy-start(f32[347,384]{1,0:T(8,128)} %get-tuple-element.40) | copy-start | bytes 1598980
  26.8 1.7 %copy-start.11 = (f32[37,384]{1,0:T(8,128)S(1)}, f32[37,384]{1,0:T(8,128)}, u32[]{:S(2)}) copy-start(f32[37,384]{1,0:T(8,128)} %get-tuple-element.39) | copy-start | bytes 170500
  26.8 1.7 %copy-start.12 = (f32[37,384]{1,0:T(8,128)S(1)}, f32[37,384]{1,0:T(8,128)}, u32[]{:S(2)}) copy-start(f32[37,384]{1,0:T(8,128)} %get-tuple-element.33) | copy-start | bytes 170500
  26.8 1.7 %copy-start.13 = (f32[37,384]{1,0:T(8,128)S(1)}, f32[37,384]{1,0:T(8,128)}, u32[]{:S(2)}) copy-start(f32[37,384]{1,0:T(8,128)} %get-tuple-element.38) | copy-start | bytes 170500
  26.8 1.7 %copy-start.15 = (f32[1,384]{1,0:T(1,128)S(1)}, f32[1,384]{1,0:T(1,128)}, u32[]{:S(2)}) copy-start(f32[1,384]{1,0:T(1,128)} %slice.270) | copy-start | bytes 4612
  33.9 1.2 %copy-start.19 = (f32[1,3,1]{1,2,0:T(1,128)S(1)}, f32[1,3,1]{1,2,0:T(1,128)}, u32[]{:S(2)}) copy-start(f32[1,3,1]{1,2,0:T(1,128)} %param.19) | copy-start | bytes 40
  33.9 1.2 %copy-start.20 = (f32[2]{0:T(128)S(1)}, f32[2]{0:T(128)}, u32[]{:S(2)}) copy-start(f32[2]{0:T(128)} %constant.78.clone) | copy-start | bytes 28
  33.9 1.3 %copy-start.16 = (f32[384,2]{0,1:T(2,128)S(1)}, f32[384,2]{0,1:T(2,128)}, u32[]{:S(2)}) copy-start(f32[384,2]{0,1:T(2,128)} %constant.76.clone) | copy-start | bytes 9220
  33.9 1.3 %copy-start.17 = (f32[384,2]{0,1:T(2,128)S(1)}, f32[384,2]{0,1:T(2,128)}, u32[]{:S(2)}) copy-start(f32[384,2]{0,1:T(2,128)} %constant.77.clone) | copy-start | bytes 9220
  34.1 2.4 %copy-start.18 = (s32[1,3]{1,0:T(1,128)S(1)}, s32[1,3]{1,0:T(1,128)}, u32[]{:S(2)}) copy-start(s32[1,3]{1,0:T(1,128)} %param.20) | copy-start | bytes 40
  34.1 2.5 %copy-start.14 = (s32[1,3,12,12]{3,0,2,1:T(1,128)S(1)}, s32[1,3,12,12]{3,0,2,1:T(1,128)}, u32[]{:S(2)}) copy-start(s32[1,3,12,12]{3,0,2,1:T(1,128)} %param.18) | copy-start | bytes 5188
  58.3 20.4 %all-to-all-start.1 = ((bf16[16,3,24,384]{3,2,1,0:T(8,128)(2,1)}), bf16[16,3,24,384]{3,2,1,0:T(8,128)(2,1)S(1)}, u32[]{:S(2)}, u32[]{:S(2)}) async-start(bf16[16,3,24,384]{3,2,1,0:T(8,128)(2,1)} %tiles.1), calls=%async_computation.1 | async-start | bytes 1769472 | tf_op jit(solution)/shard_map/all_to_all | solution.py:282
  96.3 9.0 %collective-permute-start = (bf16[320,64]{1,0:T(8,128)(2,1)S(1)}, bf16[320,64]{1,0:T(8,128)(2,1)S(1)}, u32[]{:S(2)}, u32[]{:S(2)}) collective-permute-start(bf16[320,64]{1,0:T(8,128)(2,1)S(1)} %slice.409), channel_id=1, source_target_pairs={{16,0},{32,16},{48,32},{64,48},{80,64},{96,80},{112,96},{17,1},{33... | collective-permute-start | bytes 122888 | tf_op jit(solution)/shard_map/ppermute | solution.py:303
  (2 other events, 1.7 us)

commit v2 on v1

v2 whole, which is shorter than its diff:
```python
import functools
import math

import jax
import jax.numpy as jnp
import numpy as np
from jax import lax
from jax.experimental import pallas as pl
from jax.experimental.pallas import tpu as pltpu
from jax.sharding import PartitionSpec as P

SIDE = 384
STRIDE = 320
OVERLAP = SIDE - STRIDE
GROUP_COLS = 2
PHASES = 5
CELLS = 12
WIENER = 0.1
SHIFT_ROWS, SHIFT_COLS = 37, 101
CHUNK = SIDE // 16
GROUP = 8
ROW_GROUPS = CHUNK // GROUP
TILE_GROUPS = 3 * ROW_GROUPS

COL_A = np.arange(64, 128)
COL_B = np.arange(128, 192)
COL_C = np.arange(0, 64)
NYQUIST = SIDE // 2


def cos_sin(rows, cols):
    angle = (np.outer(rows, cols) % SIDE) * (2.0 * math.pi / SIDE)
    return np.cos(angle), np.sin(angle)


def band_columns(order):
    move = order * SHIFT_COLS
    return np.concatenate([
        COL_B + move, COL_A + move, COL_B - move, COL_A - move,
        COL_C + move, [NYQUIST + move], COL_C[1:] - move,
    ])


def centre_table():
    cols = np.concatenate([COL_B, COL_A, COL_C, [NYQUIST]])
    c, s = cos_sin(np.arange(SIDE), cols)
    pad = np.zeros((SIDE, 63))
    return np.concatenate([c, pad, -s, pad], axis=1)


def last_table():
    lines = np.concatenate([COL_B, COL_A, COL_C, [NYQUIST], COL_C[1:]])
    c, s = cos_sin(lines, np.arange(SIDE))
    return np.concatenate([c, s], axis=0)


def table(values):
    return jnp.asarray(values.astype(np.float32)).astype(jnp.bfloat16)


def dot(x, w):
    return jnp.dot(x, w, preferred_element_type=jnp.float32)


def halves(x):
    high = x.astype(jnp.bfloat16)
    return high, (x - high.astype(jnp.float32)).astype(jnp.bfloat16)


def negated(x, flip):
    high, low = halves(x)
    high = dot(flip, high).astype(jnp.bfloat16)
    low = dot(flip, low).astype(jnp.bfloat16)
    return dot(high, flip) + dot(low, flip)


def fill_gains(otf_ref, apod_ref, work_ref, gains_ref):
    rows = lax.broadcasted_iota(jnp.int32, (SIDE, SIDE), 0)
    cols = lax.broadcasted_iota(jnp.int32, (SIDE, SIDE), 1)
    total = rows + cols
    flip = ((total == 0) | (total == SIDE)).astype(jnp.float32).astype(jnp.bfloat16)
    orders = range(-2, 3)

    def moved(source, order):
        if order:
            source = pltpu.roll(source, (-order * SHIFT_COLS) % SIDE, 1)[:, 0:256]
            return pltpu.roll(source, (-order * SHIFT_ROWS) % SIDE, 0)
        return source[:, 0:256]

    def fill(source, numerator, first):
        power = None
        for at, order in enumerate(orders):
            one = moved(source, order)
            work_ref[at] = one
            power = one * one if power is None else power + one * one
        scale = numerator / (WIENER + power)
        for at in range(5):
            at_rows = pl.ds(SIDE * at, SIDE)
            if first:
                gains_ref[at_rows, :] = work_ref[at] * scale
            else:
                gains_ref[at_rows, :] += work_ref[at] * scale

    fill(otf_ref[...], apod_ref[:, 0:256], True)
    fill(negated(otf_ref[...], flip), negated(apod_ref[...], flip)[:, 0:256], False)


def pack_gains(natural_ref, gains_ref):
    lane = lax.broadcasted_iota(jnp.int32, (SIDE, 128), 1)
    low = lane < 64
    nyquist = lane == 64

    def tiles(order):
        at = pl.ds(SIDE * (order + 2), SIDE)
        return natural_ref[at, 0:128], natural_ref[at, 128:256]

    for order in (1, 2):
        base = 256 * (order - 1)
        up0, up1 = tiles(order)
        down0, down1 = tiles(-order)
        gains_ref[:, base : base + 128] = jnp.where(low, up1, up0)
        gains_ref[:, base + 128 : base + 256] = jnp.where(low, down1, down0)
        rest = jnp.where(low, up0, jnp.where(nyquist, up1, pltpu.roll(down0, 64, 1)))
        gains_ref[:, 384 + 128 * order : 512 + 128 * order] = rest
    mid0, mid1 = tiles(0)
    gains_ref[:, 768:896] = jnp.where(low, mid1, mid0)
    edge = jnp.where(lane == 0, 0.5 * mid0, mid0)
    gains_ref[:, 896:1024] = jnp.where(low, edge, jnp.where(nyquist, 0.5 * mid1, 0.0))


def fill_tables(cos_ref, sin_ref, band_refs, weight_refs, fwd_ref):
    zero = jnp.zeros((), jnp.bfloat16)
    fwd_ref[0:384, 0:384] = cos_ref[...]
    fwd_ref[0:384, 384:768] = sin_ref[...]
    fwd_ref[384:768, 0:384] = zero - sin_ref[...]
    fwd_ref[384:768, 384:768] = cos_ref[...]
    upper = lax.broadcasted_iota(jnp.int32, (SIDE, 128), 1) < 65
    for (c_ref, s_ref), w_ref in zip(band_refs, weight_refs):
        w_ref[0:384, 0:384] = c_ref[...]
        w_ref[0:384, 384:768] = zero - s_ref[...]
        for tile in range(3):
            lanes = pl.ds(128 * tile, 128)
            c, s = c_ref[:, lanes], s_ref[:, lanes]
            if tile == 0:
                c, s = zero - c, zero - s
            elif tile == 2:
                c = jnp.where(upper, -c.astype(jnp.float32), c.astype(jnp.float32)).astype(jnp.bfloat16)
                s = jnp.where(upper, -s.astype(jnp.float32), s.astype(jnp.float32)).astype(jnp.bfloat16)
            w_ref[384:768, lanes] = s
            w_ref[384:768, pl.ds(384 + 128 * tile, 128)] = c


def tile_kernel(
    devices, group_count,
    names_ref, phases_ref,
    frames_hbm, masks_ref, otf_hbm, apod_hbm, rows_ref, cols_ref,
    cos_hbm, sin_hbm, c1_hbm, s1_hbm, c2_hbm, s2_hbm, w0_hbm, last_hbm,
    out_ref,
    frames_ref, otf_ref, apod_ref, cos_ref, sin_ref, c1_ref, s1_ref, c2_ref, s2_ref, w0_ref, last_ref,
    work_ref, natural_ref, gains_ref, w1_ref, w2_ref, fwd_ref, left_ref, y_ref, s_ref, t_ref, sems,
):
    slot = pl.program_id(0)
    f32, bf16 = jnp.float32, jnp.bfloat16
    k1, k2 = math.cos(2 * math.pi / 5), math.cos(4 * math.pi / 5)
    n1, n2 = math.sin(2 * math.pi / 5), math.sin(4 * math.pi / 5)
    slots = frames_ref.shape[0]

    fixed = [
        (otf_hbm, otf_ref), (apod_hbm, apod_ref), (cos_hbm, cos_ref), (sin_hbm, sin_ref),
        (c1_hbm, c1_ref), (s1_hbm, s1_ref), (c2_hbm, c2_ref), (s2_hbm, s2_ref),
        (w0_hbm, w0_ref), (last_hbm, last_ref),
    ]

    def fixed_copy(at):
        return pltpu.make_async_copy(fixed[at][0], fixed[at][1], sems.at[at])

    def frame_copy(at):
        return pltpu.make_async_copy(frames_hbm.at[at], frames_ref.at[at], sems.at[len(fixed) + at])

    @pl.when(slot == 0)
    def _():
        for at in range(len(fixed)):
            fixed_copy(at).start()
        for at in range(slots):
            frame_copy(at).start()
        line = lax.broadcasted_iota(jnp.int32, (GROUP, 128), 0)
        tags = jnp.full((GROUP, 128), -1.0, f32)
        for at in range(slots):
            tags = jnp.where(line == at, names_ref[0, at].astype(f32), tags)
        for chunk in range(devices):
            out_ref[chunk, TILE_GROUPS * slots] = tags.astype(bf16)
        fixed_copy(0).wait()
        fixed_copy(1).wait()
        fill_gains(otf_ref, apod_ref, work_ref, natural_ref)
        pack_gains(natural_ref, gains_ref)
        for at in range(2, len(fixed)):
            fixed_copy(at).wait()
        fill_tables(cos_ref, sin_ref, ((c1_ref, s1_ref), (c2_ref, s2_ref)), (w1_ref, w2_ref), fwd_ref)

    for at in range(slots):
        @pl.when(slot == at)
        def _():
            frame_copy(at).wait()

    cell_row = lax.broadcasted_iota(jnp.int32, (CELLS, SIDE), 0)
    cell_col = lax.broadcasted_iota(jnp.int32, (CELLS, SIDE), 1) // (SIDE // CELLS)
    spread = (cell_row == cell_col).astype(f32).astype(bf16)
    flags = dot(masks_ref[0].astype(f32).astype(bf16), spread)

    phase = jnp.full((GROUP, 128), phases_ref[slot, 0], f32)
    turns = [[fn(order * phase)[0:1, 0:1] for fn in (jnp.cos, jnp.sin)] for order in (1.0, 2.0)]

    for cell in range(CELLS):
        rows = pl.ds(32 * cell, 32)
        flag = flags[cell : cell + 1, :]
        f = [frames_ref[slot, p, rows, :].astype(f32) * flag for p in range(PHASES)]
        a1, d1, a2, d2 = f[1] + f[4], f[1] - f[4], f[2] + f[3], f[2] - f[3]
        left_ref[rows, 1536:1920] = ((f[0] + a1 + a2) * (1.0 / PHASES)).astype(bf16)
        for at, (a, b) in enumerate((
            (f[0] + k1 * a1 + k2 * a2, n1 * d1 + n2 * d2),
            (f[0] + k2 * a1 + k1 * a2, n2 * d1 - n1 * d2),
        )):
            turn_c, turn_s = turns[at]
            row_c, row_s = rows_ref[rows, 2 + 2 * at : 3 + 2 * at], rows_ref[rows, 3 + 2 * at : 4 + 2 * at]
            c = turn_c * row_c - turn_s * row_s
            s = turn_s * row_c + turn_c * row_s
            left_ref[rows, 768 * at : 768 * at + 384] = (c * a - s * b).astype(bf16)
            left_ref[rows, 768 * at + 384 : 768 * at + 768] = (c * b + s * a).astype(bf16)

    for at, w_ref in enumerate((w1_ref, w2_ref)):
        columns = (256 * at, 256 * at + 128, 512 + 128 * at)
        for part in range(3):
            r = dot(left_ref[:, 768 * at : 768 * at + 768], w_ref[:, 256 * part : 256 * part + 256]).astype(bf16)
            for half in range(2):
                tile = 2 * part + half
                base = 384 if tile >= 3 else 0
                col = columns[tile % 3]
                y_ref[base : base + 384, col : col + 128] = r[:, 128 * half : 128 * half + 128]
    for part in range(2):
        r = dot(left_ref[:, 1536:1920], w0_ref[:, 256 * part : 256 * part + 256]).astype(bf16)
        y_ref[384 * part : 384 * part + 384, 768:1024] = r

    for half in range(2):
        rows = pl.ds(384 * half, 384)
        lhs = fwd_ref[rows, :]
        sign = 1.0 - 2.0 * half

        def part(n):
            lanes = pl.ds(256 * n, 256)
            return dot(lhs, y_ref[:, lanes]) * gains_ref[:, lanes]

        d = part(0)
        t_ref[:, 0:128] = d[:, 0:128] + d[:, 128:256]
        d = part(1)
        t_ref[:, 0:128] += d[:, 0:128] + d[:, 128:256]
        d = part(2)
        t_ref[:, 128:256] = d[:, 0:128] + d[:, 128:256]
        d = part(3)
        s_ref[rows, :] = (sign * (t_ref[...] + d)).astype(bf16)

    mid_real = dot(fwd_ref[0:384, :], s_ref[...]).astype(bf16)
    mid_imag = dot(fwd_ref[384:768, :], s_ref[...]).astype(bf16)
    picture = dot(mid_real, last_ref[0:256, :]) + dot(mid_imag, last_ref[256:512, :])
    name = names_ref[0, slot]
    row_last = name >= GROUP_COLS * (devices - 1)
    col_last = (lax.axis_index("tx") == group_count - 1) & (lax.rem(name, GROUP_COLS) == GROUP_COLS - 1)
    row_ramp = rows_ref[:, 0:1] * jnp.where(row_last, 1.0, rows_ref[:, 1:2])
    col_ramp = cols_ref[0:1, :] * jnp.where(col_last, 1.0, cols_ref[1:2, :])
    weighted = picture * row_ramp * col_ramp
    for part in range(SIDE // GROUP):
        chunk, i = part // ROW_GROUPS, part % ROW_GROUPS
        for tile in range(3):
            piece = weighted[GROUP * part : GROUP * part + GROUP, 128 * tile : 128 * tile + 128]
            out_ref[chunk, TILE_GROUPS * slot + ROW_GROUPS * tile + i] = piece.astype(bf16)


def row_constants():
    places = np.arange(SIDE) + 0.5
    rising = np.minimum(places / OVERLAP, 1.0)
    falling = np.minimum((SIDE - places) / OVERLAP, 1.0)
    columns = [rising / (SIDE * SIDE), falling]
    for order in (1, 2):
        angle = (np.arange(SIDE) * order * SHIFT_ROWS % SIDE) * (2 * math.pi / SIDE)
        columns += [np.cos(angle) / PHASES, np.sin(angle) / PHASES]
    return np.stack(columns, axis=1), np.stack([rising, falling])


def tile_results(frames, masks, phases, names, otf, apod, devices, group_count):
    slots = frames.shape[0]
    f32, bf16 = jnp.float32, jnp.bfloat16
    rows, cols = (jnp.asarray(one, f32) for one in row_constants())
    every = np.arange(SIDE)
    tables = [*cos_sin(every, every), *cos_sin(every, band_columns(1)), *cos_sin(every, band_columns(2))]
    tables = [table(one) for one in tables + [centre_table(), last_table()]]
    places = pl.BlockSpec(memory_space=pl.ANY)

    def whole(array):
        return pl.BlockSpec(array.shape, lambda i, *_: (0,) * array.ndim)

    def like(array):
        return pltpu.VMEM(array.shape, array.dtype)

    return pl.pallas_call(
        functools.partial(tile_kernel, devices, group_count),
        out_shape=jax.ShapeDtypeStruct((devices, TILE_GROUPS * slots + 1, GROUP, 128), bf16),
        grid_spec=pltpu.PrefetchScalarGridSpec(
            num_scalar_prefetch=2,
            grid=(slots,),
            in_specs=[
                places,
                pl.BlockSpec((1, CELLS, CELLS), lambda i, *_: (i, 0, 0)),
                places, places, whole(rows), whole(cols),
            ] + [places] * len(tables),
            out_specs=pl.BlockSpec(memory_space=pltpu.VMEM),
            scratch_shapes=[like(frames), like(otf), like(apod)] + [like(one) for one in tables] + [
                pltpu.VMEM((5, SIDE, 256), f32),
                pltpu.VMEM((5 * SIDE, 256), f32),
                pltpu.VMEM((SIDE, 1024), f32),
                pltpu.VMEM((2 * SIDE, 2 * SIDE), bf16),
                pltpu.VMEM((2 * SIDE, 2 * SIDE), bf16),
                pltpu.VMEM((2 * SIDE, 2 * SIDE), bf16),
                pltpu.VMEM((SIDE, 1920), bf16),
                pltpu.VMEM((2 * SIDE, 1024), bf16),
                pltpu.VMEM((2 * SIDE, 256), bf16),
                pltpu.VMEM((SIDE, 256), f32),
                pltpu.SemaphoreType.DMA((2 + len(tables) + slots,)),
            ],
        ),
        cost_estimate=pl.CostEstimate(flops=slots * 3_000_000_000, bytes_accessed=12_000_000, transcendentals=0),
        name="tiles",
    )(names, phases, frames, masks, otf, apod, rows, cols, *tables)


def pick_kernel(slots, devices, in_ref, out_ref, where_ref, place_ref, sem):
    me = lax.axis_index("ty")
    per_device = TILE_GROUPS * slots + 1
    line = lax.broadcasted_iota(jnp.int32, (GROUP, 128), 0)
    lane = lax.broadcasted_iota(jnp.int32, (GROUP, 128), 1).astype(jnp.float32)
    place = jnp.zeros((GROUP, 128), jnp.int32)
    for source in range(devices):
        tags = in_ref[source, per_device - 1].astype(jnp.float32)
        place += jnp.where(tags == lane, per_device * source + TILE_GROUPS * line, 0)
    where_ref[...] = jnp.sum(place, axis=0, keepdims=True)
    copy = pltpu.make_async_copy(where_ref, place_ref, sem)
    copy.start()
    copy.wait()

    for i in range(ROW_GROUPS):
        ahead = (ROW_GROUPS * me + i < OVERLAP // GROUP).astype(jnp.int32)
        for target in range(devices):
            row = target + ahead
            held = row < devices
            for col in range(GROUP_COLS):
                source = place_ref[0, GROUP_COLS * row + col]
                home = source // per_device
                group = source - per_device * home
                for tile in range(3):
                    value = in_ref[home, group + ROW_GROUPS * tile + i]
                    if target == devices - 1:
                        value = jnp.where(held, value, jnp.zeros_like(value))
                    out_ref[target, TILE_GROUPS * col + ROW_GROUPS * tile + i] = value


def picked(spread, slots):
    devices = spread.shape[0]
    return pl.pallas_call(
        functools.partial(pick_kernel, slots, devices),
        out_shape=jax.ShapeDtypeStruct((devices, GROUP_COLS * TILE_GROUPS, GROUP, 128), spread.dtype),
        in_specs=[pl.BlockSpec(memory_space=pltpu.VMEM)],
        out_specs=pl.BlockSpec(memory_space=pltpu.VMEM),
        scratch_shapes=[
            pltpu.VMEM((1, 128), jnp.int32), pltpu.SMEM((1, 128), jnp.int32), pltpu.SemaphoreType.DMA,
        ],
        name="pick",
    )(spread)


def folded(in_ref, col, tile):
    rows = []
    for part in range(SIDE // GROUP):
        value = in_ref[part // ROW_GROUPS, TILE_GROUPS * col + ROW_GROUPS * tile + part % ROW_GROUPS]
        rows.append(value.astype(jnp.float32))
    count = OVERLAP // GROUP
    body = rows[count:]
    for at in range(count):
        body[len(body) - count + at] = body[len(body) - count + at] + rows[at]
    return jnp.concatenate(body, axis=0)


def strip_kernel(in_ref, out_ref):
    out_ref[...] = folded(in_ref, 0, 0).astype(jnp.bfloat16)


def join_kernel(in_ref, strip_ref, out_ref):
    low = lax.broadcasted_iota(jnp.int32, (STRIDE, 128), 1) < OVERLAP
    left = [pltpu.roll(folded(in_ref, 0, tile), OVERLAP, 1) for tile in range(3)]
    right = [folded(in_ref, 1, tile) for tile in range(3)]
    out_ref[:, 0:128] = jnp.where(low, left[0], left[1])
    out_ref[:, 128:256] = jnp.where(low, left[1], left[2])
    out_ref[:, 256:384] = right[0] + jnp.where(low, left[2], 0.0)
    out_ref[:, 384:512] = right[1]
    strip = pltpu.roll(strip_ref[...].astype(jnp.float32), OVERLAP, 1)
    out_ref[:, 512:640] = right[2] + jnp.where(low, 0.0, strip)


def shards(frames, masks, phases, slot_tile, otf, apod):
    devices = lax.axis_size("ty")
    group_count = lax.axis_size("tx")
    slots = frames.shape[1]
    results = tile_results(
        frames[0, :, 0], masks[0], phases[0], slot_tile, otf, apod, devices, group_count
    )
    spread = lax.all_to_all(results, "ty", 0, 0, tiled=True)
    home = lax.all_to_all(picked(spread, slots), "ty", 0, 0, tiled=True)
    in_vmem = pl.BlockSpec(memory_space=pltpu.VMEM)
    strip = pl.pallas_call(
        strip_kernel,
        out_shape=jax.ShapeDtypeStruct((STRIDE, 128), jnp.bfloat16),
        in_specs=[in_vmem], out_specs=in_vmem, name="strip",
    )(home)
    strip = lax.ppermute(strip, "tx", [(g, g - 1) for g in range(1, group_count)])
    return pl.pallas_call(
        join_kernel,
        out_shape=jax.ShapeDtypeStruct((STRIDE, STRIDE * GROUP_COLS), jnp.float32),
        in_specs=[in_vmem, in_vmem], out_specs=in_vmem, name="join",
    )(home, strip)


def solution(mesh):
    in_specs = (
        P("tx", "ty", None, None, None, None),
        P("tx", "ty", None, None),
        P("tx", "ty", None),
        P("tx", "ty"),
        P(),
        P(),
    )
    return jax.shard_map(
        shards, mesh=mesh, in_specs=in_specs, out_specs=P("ty", "tx"), check_vma=False
    )
```

time: 108 us -> 74.9 us (0.69)
  local copies, waits for them, and re-layouts: 28.1 us -> 3.26 us
  blocking collectives: 13.5 us -> 36.9 us
  starting transfers between devices: 19.7 us -> 4.73 us
  other arithmetic: 10.8 us -> 0 us
  waiting for transfers between devices: 14.5 us -> 3.84 us
  Pallas kernels: 19.6 us -> 25.6 us
    all_to_all x1 -> x2, blocking collectives: 13.5 us -> 36.9 us  [the longest x1 22.3 us: shards(): spread = lax.all_to_all(results, 'ty', 0, 0, tiled=True)]
    slice x32 -> x0, local copies, waits for them, and re-layouts: 17 us -> none  [the longest x10 10.9 us: negated(): return jnp.roll(array[::-1, ::-1], (1, 1), (0, 1))]
    all_to_all x2 -> x0, starting transfers between devices: 14.2 us -> none  [the longest x1 7.57 us: shards(): lax.all_to_all(jnp.broadcast_to(own[None], (devices, slots)), 'ty', 0, 0,...]
    all_to_all x2 -> x0, waiting for transfers between devices: 11.2 us -> none  [the longest x1 11.2 us: shards(): spread = lax.all_to_all(results, 'ty', 0, 0, tiled=True)]
    pallas_call x2 -> x4, Pallas kernels: 19.6 us -> 25.6 us  [the longest x1 18.5 us: tile_results(): pl.pallas_call(functools.partial(tile_kernel, devices, group_count), out_...]
    add x6 -> x0, other arithmetic: 4.74 us -> none  [the longest x3 4.56 us: band_gains(): gains[m] = moved[m + halfway] * scale + back[halfway - m] * back_scale]
    concatenate x1 -> x0, local copies, waits for them, and re-layouts: 3.38 us -> none  [band_gains(): return jnp.concatenate(tiles, axis=1)]
    concatenate x5 -> x0, other arithmetic: 3.16 us -> none  [the longest x3 1.76 us: weights(): jnp.roll(base, (-sign * m * SHIFT_ROWS, -sign * m * SHIFT_COLS), (0, 1))]
  transfers between devices with their start and end apart: 3 -> 1, of which waited for: 2 -> 1; matrix products, arithmetic and copies ran while one was open for 31% -> 0% of each run, Pallas kernels for 16% -> 0%
where the time goes in v2:
time: 74.9 us; the launch traced here: 74.4 us
  blocking collectives  36.9 us (49%)
  Pallas kernels  25.6 us (34%)
  starting transfers between devices  4.73 us (6%)
  waiting for transfers between devices  3.84 us (5%)
  local copies, waits for them, and re-layouts  3.26 us (4%)
    all_to_all x1, blocking collectives, shards(): spread = lax.all_to_all(results, 'ty', 0, 0, tiled=True)  22.3 us
    pallas_call x1, Pallas kernels, tile_results(): pl.pallas_call(functools.partial(tile_kernel, devices, group_count), out_...  18.5 us
    all_to_all x1, blocking collectives, shards(): home = lax.all_to_all(picked(spread, slots), 'ty', 0, 0, tiled=True)  14.6 us
    ppermute x1, starting transfers between devices, shards(): lax.ppermute(strip, 'tx', [(g, g - 1) for g in range(1, group_count)])  4.73 us
    ppermute x1, waiting for transfers between devices, shards(): lax.ppermute(strip, 'tx', [(g, g - 1) for g in range(1, group_count)])  3.84 us
    pallas_call x1, Pallas kernels, picked(): pl.pallas_call(functools.partial(pick_kernel, slots, devices), out_shape=...  3.22 us
    pallas_call x1, Pallas kernels, shards(): pl.pallas_call(join_kernel, out_shape=jax.ShapeDtypeStruct((STRIDE, STRID...  2.14 us
    unnamed x3, local copies, waits for them, and re-layouts  1.96 us
  transfers between devices with their start and end apart: 1, of which 1 were waited for; matrix products, arithmetic and copies ran while one was open for 0% of the time, Pallas kernels for 0%

profile of v2, /device:TPU:1, one launch (start us, length us, event | category | flops | bytes accessed | tf_op | source)
XLA Modules:
  0.0 74.4 jit_solution(16092447119131856654)
XLA Ops:
  0.0 1.3 %copy.17.phases_ref = f32[3,1]{1,0:T(4,128)} copy(f32[3,1]{0,1:T(1,128)} %bitcast.6) | data formatting | bytes 24 | tf_op jit(solution)/shard_map/squeeze | solution.py:411
  1.3 1.3 %copy.20 = s32[1,3,12,12]{3,2,0,1:T(8,128)} copy(s32[1,3,12,12]{3,0,2,1:T(1,128)} %param.17) | data formatting | bytes 3456
  2.6 18.5 %tiles.1 = bf16[16,28,8,128]{3,2,1,0:T(8,128)(2,1)} custom-call(s32[1,3]{1,0:T(1,128)} %names_ref.1, f32[3,1]{1,0:T(4,128)} %copy.17.phases_ref, bf16[3,5,384,384]{3,2,1,0:T(8,128)(2,1)} %bitcast.7, s32[3,12,12]{2,1,0:T(8,128)} %bitcast.5, f32[384,384]{1,0:T(8,128)} %otf_hbm.1, f32[384,384]{1,0:T(8,128)} %apod_hbm.1, f32[384,6]{1,0:T(8,128)} %constant.20.clone.rows_ref, ...), custom_call_target="tpu_custom_call" | custom-call | flops 8999999488 | bytes 12000000 | tf_op jit(solution)/shard_map/tiles/pallas_call | solution.py:303
  21.2 22.3 %all_to_all.10.in_ref = bf16[16,28,8,128]{3,2,1,0:T(8,128)(2,1)} all-to-all(bf16[16,28,8,128]{3,2,1,0:T(8,128)(2,1)} %tiles.1), channel_id=1, replica_groups=mesh['tx'=8,'ty'=16] {'ty'}, dimensions={0} | all-to-all | bytes 1835008 | tf_op jit(solution)/shard_map/all_to_all | solution.py:413
  43.5 3.2 %pick.1 = bf16[16,18,8,128]{3,2,1,0:T(8,128)(2,1)} custom-call(bf16[16,28,8,128]{3,2,1,0:T(8,128)(2,1)} %all_to_all.10.in_ref), custom_call_target="tpu_custom_call" | custom-call | tf_op jit(solution)/shard_map/pick/pallas_call | solution.py:366
  46.7 14.6 %all_to_all.11.in_ref = bf16[16,18,8,128]{3,2,1,0:T(8,128)(2,1)} all-to-all(bf16[16,18,8,128]{3,2,1,0:T(8,128)(2,1)} %pick.1), channel_id=1, replica_groups=mesh['tx'=8,'ty'=16] {'ty'}, dimensions={0} | all-to-all | bytes 1179648 | tf_op jit(solution)/shard_map/all_to_all | solution.py:414
  61.3 1.7 %strip.1 = bf16[320,128]{1,0:T(8,128)(2,1)} custom-call(bf16[16,18,8,128]{3,2,1,0:T(8,128)(2,1)} %all_to_all.11.in_ref), custom_call_target="tpu_custom_call" | custom-call | tf_op jit(solution)/shard_map/strip/pallas_call | solution.py:416
  63.0 4.7 %collective-permute-start = (bf16[320,128]{1,0:T(8,128)(2,1)}, bf16[320,128]{1,0:T(8,128)(2,1)S(1)}, u32[]{:S(2)}, u32[]{:S(2)}) collective-permute-start(bf16[320,128]{1,0:T(8,128)(2,1)} %strip.1), channel_id=1, source_target_pairs={{16,0},{32,16},{48,32},{64,48},{80,64},{96,80},{112,96},{17,1},{33... | collective-permute-start | bytes 245768 | tf_op jit(solution)/shard_map/ppermute | solution.py:421
  67.8 3.8 %collective-permute-done.strip_ref = bf16[320,128]{1,0:T(8,128)(2,1)S(1)} collective-permute-done((bf16[320,128]{1,0:T(8,128)(2,1)}, bf16[320,128]{1,0:T(8,128)(2,1)S(1)}, u32[]{:S(2)}, u32[]{:S(2)}) %collective-permute-start) | collective-permute-done | bytes 81952 | tf_op jit(solution)/shard_map/ppermute | solution.py:421
  71.6 0.0 copy-start
  71.6 0.6 copy-done
  72.2 2.1 %join.1 = f32[320,640]{1,0:T(8,128)} custom-call(bf16[16,18,8,128]{3,2,1,0:T(8,128)(2,1)} %all_to_all.11.in_ref, bf16[320,128]{1,0:T(8,128)(2,1)} %copy-done), custom_call_target="tpu_custom_call" | custom-call | tf_op jit(solution)/shard_map/join/pallas_call | solution.py:422
Async XLA Ops:
  63.0 8.6 %collective-permute-start = (bf16[320,128]{1,0:T(8,128)(2,1)}, bf16[320,128]{1,0:T(8,128)(2,1)S(1)}, u32[]{:S(2)}, u32[]{:S(2)}) collective-permute-start(bf16[320,128]{1,0:T(8,128)(2,1)} %strip.1), channel_id=1, source_target_pairs={{16,0},{32,16},{48,32},{64,48},{80,64},{96,80},{112,96},{17,1},{33... | collective-permute-start | bytes 245768 | tf_op jit(solution)/shard_map/ppermute | solution.py:421
  71.6 0.6 copy-start

commit v3 on v2

--- a/solution.py
+++ b/solution.py
@@ -18,6 +18,7 @@
 WIENER = 0.1
 SHIFT_ROWS, SHIFT_COLS = 37, 101
 CHUNK = SIDE // 16
+SMALL_VMEM = 4 << 20
 GROUP = 8
 ROW_GROUPS = CHUNK // GROUP
 TILE_GROUPS = 3 * ROW_GROUPS
@@ -205,9 +206,10 @@
     cell_row = lax.broadcasted_iota(jnp.int32, (CELLS, SIDE), 0)
     cell_col = lax.broadcasted_iota(jnp.int32, (CELLS, SIDE), 1) // (SIDE // CELLS)
     spread = (cell_row == cell_col).astype(f32).astype(bf16)
-    flags = dot(masks_ref[0].astype(f32).astype(bf16), spread)
-
-    phase = jnp.full((GROUP, 128), phases_ref[slot, 0], f32)
+    held = jnp.concatenate([masks_ref[0, row] for row in range(CELLS)], axis=0)
+    flags = dot(held.astype(f32).astype(bf16), spread)
+
+    phase = jnp.full((GROUP, 128), phases_ref[0, slot], f32)
     turns = [[fn(order * phase)[0:1, 0:1] for fn in (jnp.cos, jnp.sin)] for order in (1.0, 2.0)]
 
     for cell in range(CELLS):
@@ -308,7 +310,7 @@
             grid=(slots,),
             in_specs=[
                 places,
-                pl.BlockSpec((1, CELLS, CELLS), lambda i, *_: (i, 0, 0)),
+                pl.BlockSpec((1, CELLS, 1, CELLS), lambda i, *_: (i, 0, 0, 0)),
                 places, places, whole(rows), whole(cols),
             ] + [places] * len(tables),
             out_specs=pl.BlockSpec(memory_space=pltpu.VMEM),
@@ -338,7 +340,7 @@
     lane = lax.broadcasted_iota(jnp.int32, (GROUP, 128), 1).astype(jnp.float32)
     place = jnp.zeros((GROUP, 128), jnp.int32)
     for source in range(devices):
-        tags = in_ref[source, per_device - 1].astype(jnp.float32)
+        tags = in_ref[per_device * source + per_device - 1].astype(jnp.float32)
         place += jnp.where(tags == lane, per_device * source + TILE_GROUPS * line, 0)
     where_ref[...] = jnp.sum(place, axis=0, keepdims=True)
     copy = pltpu.make_async_copy(where_ref, place_ref, sem)
@@ -349,36 +351,35 @@
         ahead = (ROW_GROUPS * me + i < OVERLAP // GROUP).astype(jnp.int32)
         for target in range(devices):
             row = target + ahead
-            held = row < devices
             for col in range(GROUP_COLS):
-                source = place_ref[0, GROUP_COLS * row + col]
-                home = source // per_device
-                group = source - per_device * home
+                source = place_ref[0, GROUP_COLS * row + col] + i
                 for tile in range(3):
-                    value = in_ref[home, group + ROW_GROUPS * tile + i]
+                    value = in_ref[source + ROW_GROUPS * tile]
                     if target == devices - 1:
-                        value = jnp.where(held, value, jnp.zeros_like(value))
-                    out_ref[target, TILE_GROUPS * col + ROW_GROUPS * tile + i] = value
+                        value = jnp.where(row < devices, value, jnp.zeros_like(value))
+                    out_ref[TILE_GROUPS * (GROUP_COLS * target + col) + ROW_GROUPS * tile + i] = value
 
 
 def picked(spread, slots):
     devices = spread.shape[0]
-    return pl.pallas_call(
+    chosen = pl.pallas_call(
         functools.partial(pick_kernel, slots, devices),
-        out_shape=jax.ShapeDtypeStruct((devices, GROUP_COLS * TILE_GROUPS, GROUP, 128), spread.dtype),
+        out_shape=jax.ShapeDtypeStruct((devices * GROUP_COLS * TILE_GROUPS, GROUP, 128), spread.dtype),
         in_specs=[pl.BlockSpec(memory_space=pltpu.VMEM)],
         out_specs=pl.BlockSpec(memory_space=pltpu.VMEM),
         scratch_shapes=[
             pltpu.VMEM((1, 128), jnp.int32), pltpu.SMEM((1, 128), jnp.int32), pltpu.SemaphoreType.DMA,
         ],
+        compiler_params=pltpu.CompilerParams(vmem_limit_bytes=SMALL_VMEM),
         name="pick",
-    )(spread)
-
-
-def folded(in_ref, col, tile):
+    )(spread.reshape(-1, GROUP, 128))
+    return chosen.reshape(devices, -1, GROUP, 128)
+
+
+def folded(in_ref, base):
     rows = []
     for part in range(SIDE // GROUP):
-        value = in_ref[part // ROW_GROUPS, TILE_GROUPS * col + ROW_GROUPS * tile + part % ROW_GROUPS]
+        value = in_ref[part // ROW_GROUPS, base + part % ROW_GROUPS]
         rows.append(value.astype(jnp.float32))
     count = OVERLAP // GROUP
     body = rows[count:]
@@ -387,19 +388,15 @@
     return jnp.concatenate(body, axis=0)
 
 
-def strip_kernel(in_ref, out_ref):
-    out_ref[...] = folded(in_ref, 0, 0).astype(jnp.bfloat16)
-
-
 def join_kernel(in_ref, strip_ref, out_ref):
     low = lax.broadcasted_iota(jnp.int32, (STRIDE, 128), 1) < OVERLAP
-    left = [pltpu.roll(folded(in_ref, 0, tile), OVERLAP, 1) for tile in range(3)]
-    right = [folded(in_ref, 1, tile) for tile in range(3)]
+    left = [pltpu.roll(folded(in_ref, ROW_GROUPS * tile), OVERLAP, 1) for tile in range(3)]
+    right = [folded(in_ref, TILE_GROUPS + ROW_GROUPS * tile) for tile in range(3)]
     out_ref[:, 0:128] = jnp.where(low, left[0], left[1])
     out_ref[:, 128:256] = jnp.where(low, left[1], left[2])
     out_ref[:, 256:384] = right[0] + jnp.where(low, left[2], 0.0)
     out_ref[:, 384:512] = right[1]
-    strip = pltpu.roll(strip_ref[...].astype(jnp.float32), OVERLAP, 1)
+    strip = pltpu.roll(folded(strip_ref, 0), OVERLAP, 1)
     out_ref[:, 512:640] = right[2] + jnp.where(low, 0.0, strip)
 
 
@@ -408,21 +405,18 @@
     group_count = lax.axis_size("tx")
     slots = frames.shape[1]
     results = tile_results(
-        frames[0, :, 0], masks[0], phases[0], slot_tile, otf, apod, devices, group_count
+        frames[0, :, 0], masks[0][:, :, None, :], phases[:, :, 0], slot_tile, otf, apod, devices, group_count
     )
     spread = lax.all_to_all(results, "ty", 0, 0, tiled=True)
     home = lax.all_to_all(picked(spread, slots), "ty", 0, 0, tiled=True)
+    strip = lax.ppermute(home[:, :ROW_GROUPS], "tx", [(g, g - 1) for g in range(1, group_count)])
     in_vmem = pl.BlockSpec(memory_space=pltpu.VMEM)
-    strip = pl.pallas_call(
-        strip_kernel,
-        out_shape=jax.ShapeDtypeStruct((STRIDE, 128), jnp.bfloat16),
-        in_specs=[in_vmem], out_specs=in_vmem, name="strip",
-    )(home)
-    strip = lax.ppermute(strip, "tx", [(g, g - 1) for g in range(1, group_count)])
     return pl.pallas_call(
         join_kernel,
         out_shape=jax.ShapeDtypeStruct((STRIDE, STRIDE * GROUP_COLS), jnp.float32),
-        in_specs=[in_vmem, in_vmem], out_specs=in_vmem, name="join",
+        in_specs=[in_vmem, in_vmem], out_specs=in_vmem,
+        compiler_params=pltpu.CompilerParams(vmem_limit_bytes=SMALL_VMEM),
+        name="join",
     )(home, strip)
 
 

time: 74.9 us -> 65.1 us (0.87)
  Pallas kernels: 25.6 us -> 20.4 us
  local copies, waits for them, and re-layouts: 3.26 us -> 0.01 us
  blocking collectives: 36.9 us -> 35.6 us
    pallas_call x1, Pallas kernels: 3.22 us -> 0.75 us  [picked(): pl.pallas_call(functools.partial(pick_kernel, slots, devices), out_shape=...]
    unnamed x3 -> x0, local copies, waits for them, and re-layouts: 1.96 us -> none
    pallas_call x1 -> x0, Pallas kernels: 1.72 us -> none  [shards(): pl.pallas_call(strip_kernel, out_shape=jax.ShapeDtypeStruct((STRIDE, 128)...]
    squeeze x1 -> x0, local copies, waits for them, and re-layouts: 1.31 us -> none  [shards(): phases[0]]
    all_to_all x1, blocking collectives: 14.6 us -> 13.3 us  [shards(): home = lax.all_to_all(picked(spread, slots), 'ty', 0, 0, tiled=True)]
    pallas_call x1, Pallas kernels: 2.14 us -> 1.07 us  [shards(): pl.pallas_call(join_kernel, out_shape=jax.ShapeDtypeStruct((STRIDE, STRID...]
where the time goes in v3:
time: 65.1 us; the launch traced here: 64.8 us
  blocking collectives  35.6 us (55%)
  Pallas kernels  20.4 us (31%)
  starting transfers between devices  5.04 us (8%)
  waiting for transfers between devices  3.84 us (6%)
    all_to_all x1, blocking collectives, shards(): spread = lax.all_to_all(results, 'ty', 0, 0, tiled=True)  22.2 us
    pallas_call x1, Pallas kernels, tile_results(): pl.pallas_call(functools.partial(tile_kernel, devices, group_count), out_...  18.5 us
    all_to_all x1, blocking collectives, shards(): home = lax.all_to_all(picked(spread, slots), 'ty', 0, 0, tiled=True)  13.3 us
    ppermute x1, starting transfers between devices, shards(): lax.ppermute(home[:, :ROW_GROUPS], 'tx', [(g, g - 1) for g in range(1, gr...  5.04 us
    ppermute x1, waiting for transfers between devices, shards(): lax.ppermute(home[:, :ROW_GROUPS], 'tx', [(g, g - 1) for g in range(1, gr...  3.84 us
  transfers between devices with their start and end apart: 1, of which 1 were waited for; matrix products, arithmetic and copies ran while one was open for 0% of the time, Pallas kernels for 0%

profile of v3, /device:TPU:1, one launch (start us, length us, event | category | flops | bytes accessed | tf_op | source)
XLA Modules:
  0.0 64.8 jit_solution(2775851838845285793)
XLA Ops:
  0.0 18.5 %tiles.1 = bf16[16,28,8,128]{3,2,1,0:T(8,128)(2,1)} custom-call(s32[1,3]{1,0:T(1,128)} %names_ref.1, f32[1,3]{1,0:T(1,128)} %bitcast.9, bf16[3,5,384,384]{3,2,1,0:T(8,128)(2,1)} %bitcast.7, s32[3,12,1,12]{3,2,1,0:T(1,128)} %bitcast.8, f32[384,384]{1,0:T(8,128)} %otf_hbm.1, f32[384,384]{1,0:T(8,128)} %apod_hbm.1, f32[384,6]{1,0:T(8,128)} %constant.20.clone.rows_ref, ...), custom_call_target="tpu_custom_call" | custom-call | flops 8999999488 | bytes 12000000 | tf_op jit(solution)/shard_map/tiles/pallas_call | solution.py:305
  18.5 22.2 %all_to_all.10 = bf16[16,28,8,128]{3,2,1,0:T(8,128)(2,1)S(1)} all-to-all(bf16[16,28,8,128]{3,2,1,0:T(8,128)(2,1)} %tiles.1), channel_id=1, replica_groups=mesh['tx'=8,'ty'=16] {'ty'}, dimensions={0} | all-to-all | bytes 1835008 | tf_op jit(solution)/shard_map/all_to_all | solution.py:410
  40.8 0.8 %pick.1 = bf16[288,8,128]{2,1,0:T(8,128)(2,1)S(1)} custom-call(bf16[448,8,128]{2,1,0:T(8,128)(2,1)S(1)} %bitcast.5), custom_call_target="tpu_custom_call" | custom-call | tf_op jit(solution)/shard_map/pick/pallas_call | solution.py:365
  41.5 13.3 %all_to_all.11.in_ref = bf16[16,18,8,128]{3,2,1,0:T(8,128)(2,1)S(1)} all-to-all(bf16[16,18,8,128]{3,2,1,0:T(8,128)(2,1)S(1)} %bitcast.6), channel_id=1, replica_groups=mesh['tx'=8,'ty'=16] {'ty'}, dimensions={0} | all-to-all | bytes 1179648 | tf_op jit(solution)/shard_map/all_to_all | solution.py:411
  54.9 5.0 %collective-permute-start = (bf16[16,3,8,128]{3,2,1,0:T(8,128)(2,1)S(1)}, bf16[16,3,8,128]{3,2,1,0:T(8,128)(2,1)S(1)}, u32[]{:S(2)}, u32[]{:S(2)}) collective-permute-start(bf16[16,3,8,128]{3,2,1,0:T(8,128)(2,1)S(1)} %slice.4), channel_id=1, source_target_pairs={{16,0},{32,16},{48,32},{64,48},{80,64},{96,80},{112,96},{17,1},{33... | collective-permute-start | bytes 294920 | tf_op jit(solution)/shard_map/ppermute | solution.py:412
  59.9 3.8 %collective-permute-done.strip_ref = bf16[16,3,8,128]{3,2,1,0:T(8,128)(2,1)S(1)} collective-permute-done((bf16[16,3,8,128]{3,2,1,0:T(8,128)(2,1)S(1)}, bf16[16,3,8,128]{3,2,1,0:T(8,128)(2,1)S(1)}, u32[]{:S(2)}, u32[]{:S(2)}) %collective-permute-start) | collective-permute-done | bytes 98336 | tf_op jit(solution)/shard_map/ppermute | solution.py:412
  63.8 1.1 %join.1 = f32[320,640]{1,0:T(8,128)} custom-call(bf16[16,18,8,128]{3,2,1,0:T(8,128)(2,1)S(1)} %all_to_all.11.in_ref, bf16[16,3,8,128]{3,2,1,0:T(8,128)(2,1)S(1)} %collective-permute-done.strip_ref), custom_call_target="tpu_custom_call" | custom-call | tf_op jit(solution)/shard_map/join/pallas_call | solution.py:414
  (1 shorter events, 0.0 us)
Async XLA Ops:
  54.9 8.9 %collective-permute-start = (bf16[16,3,8,128]{3,2,1,0:T(8,128)(2,1)S(1)}, bf16[16,3,8,128]{3,2,1,0:T(8,128)(2,1)S(1)}, u32[]{:S(2)}, u32[]{:S(2)}) collective-permute-start(bf16[16,3,8,128]{3,2,1,0:T(8,128)(2,1)S(1)} %slice.4), channel_id=1, source_target_pairs={{16,0},{32,16},{48,32},{64,48},{80,64},{96,80},{112,96},{17,1},{33... | collective-permute-start | bytes 294920 | tf_op jit(solution)/shard_map/ppermute | solution.py:412

commit v4 on v3

v4 whole, which is shorter than its diff:
```python
import functools
import math

import jax
import jax.numpy as jnp
import numpy as np
from jax import lax
from jax.experimental import pallas as pl
from jax.experimental.pallas import tpu as pltpu
from jax.sharding import PartitionSpec as P

SIDE = 384
STRIDE = 320
OVERLAP = SIDE - STRIDE
GROUP_COLS = 2
PHASES = 5
CELLS = 12
WIENER = 0.1
SHIFT_ROWS, SHIFT_COLS = 37, 101
CHUNK = SIDE // 16
SMALL_VMEM = 4 << 20
GROUP = 8
ROW_GROUPS = CHUNK // GROUP
TILE_GROUPS = 3 * ROW_GROUPS

NYQUIST = SIDE // 2
THIRD = SIDE // 3
HALF = SIDE // 2
BY_THREE = [np.arange(rest, HALF, 3) for rest in range(3)]


def cos_sin(rows, cols):
    angle = (np.outer(rows, cols) % SIDE) * (2.0 * math.pi / SIDE)
    return np.cos(angle), np.sin(angle)


def plus(cols):
    c, s = cos_sin(np.arange(THIRD), cols)
    return np.concatenate([c, s]), np.concatenate([-s, c])


def minus(cols):
    c, s = cos_sin(np.arange(THIRD), cols)
    return np.concatenate([c, -s]), np.concatenate([-s, -c])


def beside(blocks):
    return np.concatenate([b[0] for b in blocks] + [b[1] for b in blocks], axis=1)


def column_class(order, rest):
    return (rest - order * SHIFT_COLS) % 3


def first_tables():
    tables = []
    for order in (1, 2):
        move = order * SHIFT_COLS
        for rest in range(3):
            at = column_class(order, rest)
            if at == 0:
                blocks = [
                    plus(BY_THREE[0] + move), plus(np.array([NYQUIST + move])), minus(BY_THREE[0][1:] - move)
                ]
            elif at == 1:
                blocks = [plus(BY_THREE[1] + move), minus(BY_THREE[2] - move)]
            else:
                blocks = [minus(BY_THREE[1] - move), plus(BY_THREE[2] + move)]
            tables.append(beside(blocks))
    tables.append(beside([plus(BY_THREE[1]), minus(BY_THREE[2])]))
    blank = np.zeros((2 * THIRD, 63))
    tables.append(beside([plus(BY_THREE[0]), plus(np.array([NYQUIST])), (blank, blank)])[:THIRD])
    return np.concatenate(tables)


def row_tables():
    every = np.arange(HALF)
    tables = []
    for rows, cols in ((2 * every, every), (2 * every + 1, every)):
        c, s = cos_sin(rows, cols)
        tables.append(np.block([[c, s], [-s, c]]))
    return np.concatenate(tables)


def last_table():
    lines = np.concatenate([BY_THREE[1], BY_THREE[2], BY_THREE[0], [NYQUIST], BY_THREE[0][1:]])
    c, s = cos_sin(lines, np.arange(SIDE))
    return np.concatenate([c, s], axis=0)


def table(values):
    return jnp.asarray(values.astype(np.float32)).astype(jnp.bfloat16)


def dot(x, w):
    return jnp.dot(x, w, preferred_element_type=jnp.float32)


def halves(x):
    high = x.astype(jnp.bfloat16)
    return high, (x - high.astype(jnp.float32)).astype(jnp.bfloat16)


def negating(x_ref, flip, half_ref, back_ref):
    width = back_ref.shape[1]

    def over_rows(part):
        lanes = pl.ds(256 * part, 256)
        half_ref[:, lanes] = dot(flip, half_ref[:, lanes]).astype(jnp.bfloat16)

    def split():
        high, low = halves(x_ref[...])
        half_ref[:, 0:SIDE] = high
        half_ref[:, SIDE : 2 * SIDE] = low
        over_rows(0)

    def over_columns(low, high):
        here = flip[:, low:high]
        back_ref[:, low:high] = dot(half_ref[:, 0:SIDE], here) + dot(half_ref[:, SIDE : 2 * SIDE], here)

    steps = [split, functools.partial(over_rows, 1), functools.partial(over_rows, 2)]
    steps.append(functools.partial(over_columns, 0, 256))
    if width > 256:
        steps.append(functools.partial(over_columns, 256, width))
    return steps


def flip_matrix():
    rows = lax.broadcasted_iota(jnp.int32, (SIDE, SIDE), 0)
    cols = lax.broadcasted_iota(jnp.int32, (SIDE, SIDE), 1)
    total = rows + cols
    return ((total == 0) | (total == SIDE)).astype(jnp.float32).astype(jnp.bfloat16)


def class_matrix():
    rows = lax.broadcasted_iota(jnp.int32, (256, 256), 0)
    lane = lax.broadcasted_iota(jnp.int32, (256, 256), 1)
    wanted = jnp.where(lane < 64, 3 * lane + 1, jnp.where(lane < 128, 3 * lane - 190, 3 * lane - 384))
    wanted = jnp.where(lane == NYQUIST, NYQUIST, jnp.where(lane > NYQUIST, -1, wanted))
    return (rows == wanted).astype(jnp.float32).astype(jnp.bfloat16)


def filling(source_ref, numerator_ref, work_ref, gains_ref, first):
    def move(at):
        order = at - 2
        one = source_ref[...]
        if order:
            one = pltpu.roll(one, (-order * SHIFT_COLS) % SIDE, 1)[:, 0:256]
            one = pltpu.roll(one, (-order * SHIFT_ROWS) % SIDE, 0)
        work_ref[at] = one[:, 0:256]

    def scale(part):
        rows = pl.ds(128 * part, 128)
        power = WIENER + sum(work_ref[at, rows, :] * work_ref[at, rows, :] for at in range(5))
        weight = numerator_ref[rows, 0:256] / power
        for at in range(5):
            there = pl.ds(SIDE * at + 128 * part, 128)
            if first:
                gains_ref[there, :] = work_ref[at, rows, :] * weight
            else:
                gains_ref[there, :] += work_ref[at, rows, :] * weight

    return [functools.partial(move, at) for at in range(5)] + [functools.partial(scale, at) for at in range(3)]


def interleaved(few, many):
    done = 0
    for at, step in enumerate(few):
        step()
        until = (at + 1) * len(many) // len(few)
        for other in many[done:until]:
            other()
        done = until


def pack_gains(work_ref, gains_ref):
    lane = lax.broadcasted_iota(jnp.int32, (HALF, 128), 1)
    low = lane < 64
    nyquist = lane == 64
    for odd in range(2):
        rows = pl.ds(HALF * odd, HALF)

        def tiles(order):
            base = 2 * SIDE * (order + 2) + odd
            return tuple(work_ref[pl.ds(base + at, HALF, stride=2), :] for at in (0, SIDE))

        for order in (1, 2):
            base = 256 * (order - 1)
            up0, up1 = tiles(order)
            down0, down1 = tiles(-order)
            gains_ref[rows, base : base + 128] = jnp.where(low, up0, down0)
            gains_ref[rows, base + 128 : base + 256] = jnp.where(low, down0, up0)
            rest = jnp.where(low, up1, jnp.where(nyquist, up1, pltpu.roll(down1, 64, 1)))
            gains_ref[rows, 384 + 128 * order : 512 + 128 * order] = rest
        mid0, mid1 = tiles(0)
        gains_ref[rows, 768:896] = mid0
        edge = jnp.where(lane == 0, 0.5 * mid1, mid1)
        gains_ref[rows, 896:1024] = jnp.where(low, edge, jnp.where(nyquist, 0.5 * mid1, 0.0))


def tile_kernel(
    devices, group_count,
    names_ref, phases_ref,
    frames_hbm, masks_hbm, otf_hbm, apod_hbm, rows_hbm, cols_hbm, first_hbm, fwd_hbm, last_hbm,
    out_hbm,
    frames_ref, masks_ref, otf_ref, apod_ref, rows_ref, cols_ref, first_ref, fwd_ref, last_ref,
    work_ref, natural_ref, sorted_ref, gains_ref, half_ref, back_ref, back_apod_ref,
    left_a_ref, left_b_ref, y_ref, s_ref, t_ref, mid_ref, out_ref, tags_ref, sems,
):
    f32, bf16 = jnp.float32, jnp.bfloat16
    k1, k2 = math.cos(2 * math.pi / 5), math.cos(4 * math.pi / 5)
    n1, n2 = math.sin(2 * math.pi / 5), math.sin(4 * math.pi / 5)
    slots = frames_ref.shape[0]

    fixed = [
        (otf_hbm, otf_ref), (apod_hbm, apod_ref), (masks_hbm, masks_ref), (rows_hbm, rows_ref),
        (cols_hbm, cols_ref), (first_hbm, first_ref), (fwd_hbm, fwd_ref), (last_hbm, last_ref),
    ]
    early = 5
    left_refs = (left_a_ref, left_b_ref)

    def fixed_copy(at):
        return pltpu.make_async_copy(fixed[at][0], fixed[at][1], sems.at[at])

    def frame_copy(at):
        return pltpu.make_async_copy(frames_hbm.at[at], frames_ref.at[at], sems.at[len(fixed) + at])

    def out_copy(at):
        there = out_hbm.at[:, pl.ds(TILE_GROUPS * at, TILE_GROUPS)]
        return pltpu.make_async_copy(out_ref.at[at], there, sems.at[len(fixed) + slots + at])

    tags_copy = pltpu.make_async_copy(
        tags_ref, out_hbm.at[:, pl.ds(TILE_GROUPS * slots, 1)], sems.at[len(fixed) + 2 * slots]
    )

    def mixing(now):
        phase = jnp.full((GROUP, 128), phases_ref[0, now], f32)
        turns = [[fn(order * phase)[0:1, 0:1] for fn in (jnp.cos, jnp.sin)] for order in (1.0, 2.0)]
        cell_row = lax.broadcasted_iota(jnp.int32, (CELLS, SIDE), 0)
        cell_col = lax.broadcasted_iota(jnp.int32, (CELLS, SIDE), 1) // (SIDE // CELLS)
        spread = (cell_row == cell_col).astype(f32).astype(bf16)
        held = jnp.concatenate([masks_ref[now, row] for row in range(CELLS)], axis=0)
        flags = dot(held.astype(f32).astype(bf16), spread)

        def thirds(x):
            a, b, c = x[:, 0:128], x[:, 128:256], x[:, 256:384]
            both = b + c
            return a + both, a - 0.5 * both, (0.5 * math.sqrt(3.0)) * (b - c)

        def step(part):
            rows = pl.ds(16 * part, 16)
            flag = jnp.broadcast_to(flags[part // 2 : part // 2 + 1, :], (16, SIDE)).astype(bf16)
            f = [(frames_ref[now, p, rows, :] * flag).astype(f32) for p in range(PHASES)]
            a1, d1, a2, d2 = f[1] + f[4], f[1] - f[4], f[2] + f[3], f[2] - f[3]

            def put(at, value):
                left_refs[now % 2][rows, 128 * at : 128 * at + 128] = value.astype(bf16)

            total, even, odd = thirds((f[0] + a1 + a2) * (1.0 / PHASES))
            put(12, even)
            put(13, -odd)
            put(14, total)
            for at, (a, b) in enumerate((
                (f[0] + k1 * a1 + k2 * a2, n1 * d1 + n2 * d2),
                (f[0] + k2 * a1 + k1 * a2, n2 * d1 - n1 * d2),
            )):
                turn_c, turn_s = turns[at]
                row_c, row_s = rows_ref[rows, 2 + 2 * at : 3 + 2 * at], rows_ref[rows, 3 + 2 * at : 4 + 2 * at]
                c = turn_c * row_c - turn_s * row_s
                s = turn_s * row_c + turn_c * row_s
                total_r, even_r, odd_r = thirds(c * a - s * b)
                total_i, even_i, odd_i = thirds(-c * b - s * a)
                put(6 * at, total_r)
                put(6 * at + 1, total_i)
                put(6 * at + 2, even_r + odd_i)
                put(6 * at + 3, even_i - odd_r)
                put(6 * at + 4, even_r - odd_i)
                put(6 * at + 5, even_i + odd_r)

        return [functools.partial(step, part) for part in range(SIDE // 16)]

    def transform(slot, waiting):
        def mix_some(count):
            for step in waiting[:count]:
                step()
            del waiting[:count]

        def put_rows(r, col):
            for half in range(2):
                top = r[0:HALF, 128 * half : 128 * half + 128]
                bottom = r[HALF:SIDE, 128 * half : 128 * half + 128]
                base = HALF * half
                y_ref[base : base + HALF, col : col + 128] = (top + bottom).astype(bf16)
                y_ref[SIDE + base : SIDE + base + HALF, col : col + 128] = (top - bottom).astype(bf16)

        for at in range(2):
            columns = (512 + 128 * at, 256 * at, 256 * at + 128)
            for rest in range(3):
                k = 768 * at + 256 * rest
                r = dot(left_refs[slot % 2][:, k : k + 256], first_ref[k : k + 256, :])
                put_rows(r, columns[column_class(at + 1, rest)])
                mix_some(1)
        put_rows(dot(left_refs[slot % 2][:, 1536:1792], first_ref[1536:1792, :]), 768)
        mix_some(1)
        put_rows(dot(left_refs[slot % 2][:, 1792:1920], first_ref[1792:1920, :]), 896)
        mix_some(1)

        for odd in range(2):
            rows = pl.ds(SIDE * odd, SIDE)
            gain_rows = pl.ds(HALF * odd, HALF)
            for n in range(4):
                lanes = pl.ds(256 * n, 256)
                product = dot(fwd_ref[rows, :], y_ref[rows, lanes])
                g = gains_ref[gain_rows, lanes]
                for half in range(2):
                    d = product[HALF * half : HALF * half + HALF] * g
                    here = pl.ds(HALF * half, HALF)
                    if n == 0:
                        t_ref[here, 0:128] = d[:, 0:128] + d[:, 128:256]
                    elif n == 1:
                        t_ref[here, 0:128] += d[:, 0:128] + d[:, 128:256]
                    elif n == 2:
                        t_ref[here, 128:256] = d[:, 0:128] + d[:, 128:256]
                    else:
                        total = t_ref[here, :] + d
                        total = -total if half > odd else total
                        base = SIDE * odd + HALF * half
                        s_ref[base : base + HALF, :] = total.astype(bf16)
                mix_some(2)

        even_part = dot(fwd_ref[0:SIDE, :], s_ref[0:SIDE, :])
        odd_part = lax.dot_general(
            fwd_ref[SIDE : 2 * SIDE, :], s_ref[SIDE : 2 * SIDE, :], (((0,), (0,)), ((), ())),
            preferred_element_type=f32,
        )
        mix_some(len(waiting))
        for half in range(2):
            e, o = even_part[HALF * half : HALF * half + HALF], odd_part[HALF * half : HALF * half + HALF]
            o = -o if half else o
            lanes = pl.ds(256 * half, 256)
            mid_ref[0:HALF, lanes] = (e + o).astype(bf16)
            mid_ref[HALF:SIDE, lanes] = (e - o).astype(bf16)
        picture = dot(mid_ref[...], last_ref[...])
        name = names_ref[0, slot]
        row_last = name >= GROUP_COLS * (devices - 1)
        col_last = (lax.axis_index("tx") == group_count - 1) & (lax.rem(name, GROUP_COLS) == GROUP_COLS - 1)
        row_ramp = rows_ref[:, 0:1] * jnp.where(row_last, 1.0, rows_ref[:, 1:2])
        col_ramp = cols_ref[0:1, :] * jnp.where(col_last, 1.0, cols_ref[1:2, :])
        weighted = picture * row_ramp * col_ramp
        for part in range(SIDE // GROUP):
            chunk, i = part // ROW_GROUPS, part % ROW_GROUPS
            for tile in range(3):
                piece = weighted[GROUP * part : GROUP * part + GROUP, 128 * tile : 128 * tile + 128]
                out_ref[slot, chunk, ROW_GROUPS * tile + i] = piece.astype(bf16)
        out_copy(slot).start()

    for at in range(early):
        fixed_copy(at).start()
    frame_copy(0).start()
    line = lax.broadcasted_iota(jnp.int32, (GROUP, 128), 0)
    tags = jnp.full((GROUP, 128), -1.0, f32)
    for at in range(slots):
        tags = jnp.where(line == at, names_ref[0, at].astype(f32), tags)
    for chunk in range(devices):
        tags_ref[chunk, 0] = tags.astype(bf16)
    tags_copy.start()
    flip = flip_matrix()
    for at in range(early):
        fixed_copy(at).wait()
    for at in range(early, len(fixed)):
        fixed_copy(at).start()
    turning = negating(otf_ref, flip, half_ref, back_ref)
    interleaved(turning, filling(otf_ref, apod_ref, work_ref, natural_ref, True))
    frame_copy(0).wait()
    for at in range(1, slots):
        frame_copy(at).start()
    interleaved(negating(apod_ref, flip, half_ref, back_apod_ref), mixing(0))
    for step in filling(back_ref, back_apod_ref, work_ref, natural_ref, False):
        step()
    classes = class_matrix()
    for at in range(5):
        rows = pl.ds(SIDE * at, SIDE)
        high, low = halves(natural_ref[rows, :])
        sorted_gains = dot(high, classes) + dot(low, classes)
        for half in range(2):
            there = pl.ds(SIDE * (2 * at + half), SIDE)
            sorted_ref[there, :] = sorted_gains[:, 128 * half : 128 * half + 128]
    pack_gains(sorted_ref, gains_ref)
    for at in range(early, len(fixed)):
        fixed_copy(at).wait()

    for slot in range(slots):
        waiting = []
        if slot + 1 < slots:
            frame_copy(slot + 1).wait()
            waiting = mixing(slot + 1)
        transform(slot, waiting)
    tags_copy.wait()
    for at in range(slots):
        out_copy(at).wait()


def row_constants():
    places = np.arange(SIDE) + 0.5
    rising = np.minimum(places / OVERLAP, 1.0)
    falling = np.minimum((SIDE - places) / OVERLAP, 1.0)
    columns = [rising / (SIDE * SIDE), falling]
    for order in (1, 2):
        angle = (np.arange(SIDE) * order * SHIFT_ROWS % SIDE) * (2 * math.pi / SIDE)
        columns += [np.cos(angle) / PHASES, np.sin(angle) / PHASES]
    return np.stack(columns, axis=1), np.stack([rising, falling])


def tile_results(frames, masks, phases, names, otf, apod, devices, group_count):
    slots = frames.shape[0]
    f32, bf16 = jnp.float32, jnp.bfloat16
    rows, cols = (jnp.asarray(one, f32) for one in row_constants())
    tables = [table(one) for one in (first_tables(), row_tables(), last_table())]
    places = pl.BlockSpec(memory_space=pl.ANY)

    def like(array):
        return pltpu.VMEM(array.shape, array.dtype)

    given = [frames, masks, otf, apod, rows, cols] + tables
    return pl.pallas_call(
        functools.partial(tile_kernel, devices, group_count),
        out_shape=jax.ShapeDtypeStruct((devices, TILE_GROUPS * slots + 1, GROUP, 128), bf16),
        in_specs=[pl.BlockSpec(memory_space=pltpu.SMEM)] * 2 + [places] * len(given),
        out_specs=places,
        scratch_shapes=[like(one) for one in given] + [
            pltpu.VMEM((5, SIDE, 256), f32),
            pltpu.VMEM((5 * SIDE, 256), f32),
            pltpu.VMEM((10 * SIDE, 128), f32),
            pltpu.VMEM((SIDE, 1024), f32),
            pltpu.VMEM((SIDE, 2 * SIDE), bf16),
            pltpu.VMEM((SIDE, SIDE), f32),
            pltpu.VMEM((SIDE, 256), f32),
            pltpu.VMEM((SIDE, 1920), bf16),
            pltpu.VMEM((SIDE, 1920), bf16),
            pltpu.VMEM((2 * SIDE, 1024), bf16),
            pltpu.VMEM((2 * SIDE, 256), bf16),
            pltpu.VMEM((SIDE, 256), f32),
            pltpu.VMEM((SIDE, 512), bf16),
            pltpu.VMEM((slots, devices, TILE_GROUPS, GROUP, 128), bf16),
            pltpu.VMEM((devices, 1, GROUP, 128), bf16),
            pltpu.SemaphoreType.DMA((len(given) + 2 * slots,)),
        ],
        cost_estimate=pl.CostEstimate(flops=slots * 2_000_000_000, bytes_accessed=10_000_000, transcendentals=0),
        name="tiles",
    )(names, phases, *given)


def pick_kernel(slots, devices, in_ref, out_ref, where_ref, place_ref, sem):
    me = lax.axis_index("ty")
    per_device = TILE_GROUPS * slots + 1
    line = lax.broadcasted_iota(jnp.int32, (GROUP, 128), 0)
    lane = lax.broadcasted_iota(jnp.int32, (GROUP, 128), 1).astype(jnp.float32)
    place = jnp.zeros((GROUP, 128), jnp.int32)
    for source in range(devices):
        tags = in_ref[per_device * source + per_device - 1].astype(jnp.float32)
        place += jnp.where(tags == lane, per_device * source + TILE_GROUPS * line, 0)
    where_ref[...] = jnp.sum(place, axis=0, keepdims=True)
    copy = pltpu.make_async_copy(where_ref, place_ref, sem)
    copy.start()
    copy.wait()

    for i in range(ROW_GROUPS):
        ahead = (ROW_GROUPS * me + i < OVERLAP // GROUP).astype(jnp.int32)
        for target in range(devices):
            row = target + ahead
            for col in range(GROUP_COLS):
                source = place_ref[0, GROUP_COLS * row + col] + i
                for tile in range(3):
                    value = in_ref[source + ROW_GROUPS * tile]
                    if target == devices - 1:
                        value = jnp.where(row < devices, value, jnp.zeros_like(value))
                    out_ref[TILE_GROUPS * (GROUP_COLS * target + col) + ROW_GROUPS * tile + i] = value


def picked(spread, slots):
    devices = spread.shape[0]
    chosen = pl.pallas_call(
        functools.partial(pick_kernel, slots, devices),
        out_shape=jax.ShapeDtypeStruct((devices * GROUP_COLS * TILE_GROUPS, GROUP, 128), spread.dtype),
        in_specs=[pl.BlockSpec(memory_space=pltpu.VMEM)],
        out_specs=pl.BlockSpec(memory_space=pltpu.VMEM),
        scratch_shapes=[
            pltpu.VMEM((1, 128), jnp.int32), pltpu.SMEM((1, 128), jnp.int32), pltpu.SemaphoreType.DMA,
        ],
        compiler_params=pltpu.CompilerParams(vmem_limit_bytes=SMALL_VMEM),
        name="pick",
    )(spread.reshape(-1, GROUP, 128))
    return chosen.reshape(devices, -1, GROUP, 128)


def folded(in_ref, base):
    rows = []
    for part in range(SIDE // GROUP):
        value = in_ref[part // ROW_GROUPS, base + part % ROW_GROUPS]
        rows.append(value.astype(jnp.float32))
    count = OVERLAP // GROUP
    body = rows[count:]
    for at in range(count):
        body[len(body) - count + at] = body[len(body) - count + at] + rows[at]
    return jnp.concatenate(body, axis=0)


def join_kernel(in_ref, strip_ref, out_ref):
    low = lax.broadcasted_iota(jnp.int32, (STRIDE, 128), 1) < OVERLAP
    left = [pltpu.roll(folded(in_ref, ROW_GROUPS * tile), OVERLAP, 1) for tile in range(3)]
    right = [folded(in_ref, TILE_GROUPS + ROW_GROUPS * tile) for tile in range(3)]
    out_ref[:, 0:128] = jnp.where(low, left[0], left[1])
    out_ref[:, 128:256] = jnp.where(low, left[1], left[2])
    out_ref[:, 256:384] = right[0] + jnp.where(low, left[2], 0.0)
    out_ref[:, 384:512] = right[1]
    strip = pltpu.roll(folded(strip_ref, 0), OVERLAP, 1)
    out_ref[:, 512:640] = right[2] + jnp.where(low, 0.0, strip)


def shards(frames, masks, phases, slot_tile, otf, apod):
    devices = lax.axis_size("ty")
    group_count = lax.axis_size("tx")
    slots = frames.shape[1]
    results = tile_results(
        frames[0, :, 0], masks[0][:, :, None, :], phases[:, :, 0], slot_tile, otf, apod, devices, group_count
    )
    spread = lax.all_to_all(results, "ty", 0, 0, tiled=True)
    home = lax.all_to_all(picked(spread, slots), "ty", 0, 0, tiled=True)
    strip = lax.ppermute(home[:, :ROW_GROUPS], "tx", [(g, g - 1) for g in range(1, group_count)])
    in_vmem = pl.BlockSpec(memory_space=pltpu.VMEM)
    return pl.pallas_call(
        join_kernel,
        out_shape=jax.ShapeDtypeStruct((STRIDE, STRIDE * GROUP_COLS), jnp.float32),
        in_specs=[in_vmem, in_vmem], out_specs=in_vmem,
        compiler_params=pltpu.CompilerParams(vmem_limit_bytes=SMALL_VMEM),
        name="join",
    )(home, strip)


def solution(mesh):
    in_specs = (
        P("tx", "ty", None, None, None, None),
        P("tx", "ty", None, None),
        P("tx", "ty", None),
        P("tx", "ty"),
        P(),
        P(),
    )
    return jax.shard_map(
        shards, mesh=mesh, in_specs=in_specs, out_specs=P("ty", "tx"), check_vma=False
    )
```

time: 65.1 us -> 63.4 us (0.974)
  Pallas kernels: 20.4 us -> 18.7 us
    pallas_call x1, Pallas kernels: 18.5 us -> 16.9 us  [tile_results(): pl.pallas_call(functools.partial(tile_kernel, devices, group_count), out_...]
where the time goes in v4:
time: 63.4 us; the launch traced here: 63.2 us
  blocking collectives  35.6 us (56%)
  Pallas kernels  18.7 us (29%)
  starting transfers between devices  5.04 us (8%)
  waiting for transfers between devices  3.81 us (6%)
    all_to_all x1, blocking collectives, shards(): spread = lax.all_to_all(results, 'ty', 0, 0, tiled=True)  22.2 us
    pallas_call x1, Pallas kernels, tile_results(): pl.pallas_call(functools.partial(tile_kernel, devices, group_count), out_...  16.9 us
    all_to_all x1, blocking collectives, shards(): home = lax.all_to_all(picked(spread, slots), 'ty', 0, 0, tiled=True)  13.3 us
    ppermute x1, starting transfers between devices, shards(): lax.ppermute(home[:, :ROW_GROUPS], 'tx', [(g, g - 1) for g in range(1, gr...  5.04 us
    ppermute x1, waiting for transfers between devices, shards(): lax.ppermute(home[:, :ROW_GROUPS], 'tx', [(g, g - 1) for g in range(1, gr...  3.81 us
  transfers between devices with their start and end apart: 1, of which 1 were waited for; matrix products, arithmetic and copies ran while one was open for 0% of the time, Pallas kernels for 0%

profile of v4, /device:TPU:1, one launch (start us, length us, event | category | flops | bytes accessed | tf_op | source)
XLA Modules:
  0.0 63.2 jit_solution(4266164381146090415)
XLA Ops:
  0.0 16.9 %tiles.1 = bf16[16,28,8,128]{3,2,1,0:T(8,128)(2,1)} custom-call(s32[1,3]{1,0:T(1,128)} %names_ref.1, f32[1,3]{1,0:T(1,128)} %bitcast.9, bf16[3,5,384,384]{3,2,1,0:T(8,128)(2,1)} %bitcast.7, s32[3,12,1,12]{3,2,1,0:T(1,128)} %bitcast.8, f32[384,384]{1,0:T(8,128)} %otf_hbm.1, f32[384,384]{1,0:T(8,128)} %apod_hbm.1, f32[384,6]{1,0:T(8,128)} %constant.10.clone.rows_hbm, ...), custom_call_target="tpu_custom_call" | custom-call | flops 6000000000 | bytes 10000000 | tf_op jit(solution)/shard_map/tiles/pallas_call | solution.py:425
  16.9 22.2 %all_to_all.10 = bf16[16,28,8,128]{3,2,1,0:T(8,128)(2,1)S(1)} all-to-all(bf16[16,28,8,128]{3,2,1,0:T(8,128)(2,1)} %tiles.1), channel_id=1, replica_groups=mesh['tx'=8,'ty'=16] {'ty'}, dimensions={0} | all-to-all | bytes 1835008 | tf_op jit(solution)/shard_map/all_to_all | solution.py:527
  39.1 0.8 %pick.1 = bf16[288,8,128]{2,1,0:T(8,128)(2,1)S(1)} custom-call(bf16[448,8,128]{2,1,0:T(8,128)(2,1)S(1)} %bitcast.5), custom_call_target="tpu_custom_call" | custom-call | tf_op jit(solution)/shard_map/pick/pallas_call | solution.py:482
  39.9 13.3 %all_to_all.11.in_ref = bf16[16,18,8,128]{3,2,1,0:T(8,128)(2,1)S(1)} all-to-all(bf16[16,18,8,128]{3,2,1,0:T(8,128)(2,1)S(1)} %bitcast.6), channel_id=1, replica_groups=mesh['tx'=8,'ty'=16] {'ty'}, dimensions={0} | all-to-all | bytes 1179648 | tf_op jit(solution)/shard_map/all_to_all | solution.py:528
  53.2 5.0 %collective-permute-start = (bf16[16,3,8,128]{3,2,1,0:T(8,128)(2,1)S(1)}, bf16[16,3,8,128]{3,2,1,0:T(8,128)(2,1)S(1)}, u32[]{:S(2)}, u32[]{:S(2)}) collective-permute-start(bf16[16,3,8,128]{3,2,1,0:T(8,128)(2,1)S(1)} %slice.4), channel_id=1, source_target_pairs={{16,0},{32,16},{48,32},{64,48},{80,64},{96,80},{112,96},{17,1},{33... | collective-permute-start | bytes 294920 | tf_op jit(solution)/shard_map/ppermute | solution.py:529
  58.3 3.8 %collective-permute-done.strip_ref = bf16[16,3,8,128]{3,2,1,0:T(8,128)(2,1)S(1)} collective-permute-done((bf16[16,3,8,128]{3,2,1,0:T(8,128)(2,1)S(1)}, bf16[16,3,8,128]{3,2,1,0:T(8,128)(2,1)S(1)}, u32[]{:S(2)}, u32[]{:S(2)}) %collective-permute-start) | collective-permute-done | bytes 98336 | tf_op jit(solution)/shard_map/ppermute | solution.py:529
  62.1 1.1 %join.1 = f32[320,640]{1,0:T(8,128)} custom-call(bf16[16,18,8,128]{3,2,1,0:T(8,128)(2,1)S(1)} %all_to_all.11.in_ref, bf16[16,3,8,128]{3,2,1,0:T(8,128)(2,1)S(1)} %collective-permute-done.strip_ref), custom_call_target="tpu_custom_call" | custom-call | tf_op jit(solution)/shard_map/join/pallas_call | solution.py:531
  (1 shorter events, 0.0 us)
Async XLA Ops:
  53.2 8.9 %collective-permute-start = (bf16[16,3,8,128]{3,2,1,0:T(8,128)(2,1)S(1)}, bf16[16,3,8,128]{3,2,1,0:T(8,128)(2,1)S(1)}, u32[]{:S(2)}, u32[]{:S(2)}) collective-permute-start(bf16[16,3,8,128]{3,2,1,0:T(8,128)(2,1)S(1)} %slice.4), channel_id=1, source_target_pairs={{16,0},{32,16},{48,32},{64,48},{80,64},{96,80},{112,96},{17,1},{33... | collective-permute-start | bytes 294920 | tf_op jit(solution)/shard_map/ppermute | solution.py:529

commit v5 on v4

--- a/solution.py
+++ b/solution.py
@@ -208,7 +208,6 @@
     left_a_ref, left_b_ref, y_ref, s_ref, t_ref, mid_ref, out_ref, tags_ref, sems,
 ):
     f32, bf16 = jnp.float32, jnp.bfloat16
-    k1, k2 = math.cos(2 * math.pi / 5), math.cos(4 * math.pi / 5)
     n1, n2 = math.sin(2 * math.pi / 5), math.sin(4 * math.pi / 5)
     slots = frames_ref.shape[0]
 
@@ -248,21 +247,23 @@
             return a + both, a - 0.5 * both, (0.5 * math.sqrt(3.0)) * (b - c)
 
         def step(part):
-            rows = pl.ds(16 * part, 16)
-            flag = jnp.broadcast_to(flags[part // 2 : part // 2 + 1, :], (16, SIDE)).astype(bf16)
+            rows = pl.ds(32 * part, 32)
+            flag = jnp.broadcast_to(flags[part : part + 1, :], (32, SIDE)).astype(bf16)
             f = [(frames_ref[now, p, rows, :] * flag).astype(f32) for p in range(PHASES)]
             a1, d1, a2, d2 = f[1] + f[4], f[1] - f[4], f[2] + f[3], f[2] - f[3]
 
             def put(at, value):
                 left_refs[now % 2][rows, 128 * at : 128 * at + 128] = value.astype(bf16)
 
-            total, even, odd = thirds((f[0] + a1 + a2) * (1.0 / PHASES))
+            both = a1 + a2
+            total, even, odd = thirds((f[0] + both) * (1.0 / PHASES))
+            base, apart = f[0] - 0.25 * both, (0.25 * math.sqrt(5.0)) * (a1 - a2)
             put(12, even)
             put(13, -odd)
             put(14, total)
             for at, (a, b) in enumerate((
-                (f[0] + k1 * a1 + k2 * a2, n1 * d1 + n2 * d2),
-                (f[0] + k2 * a1 + k1 * a2, n2 * d1 - n1 * d2),
+                (base + apart, n1 * d1 + n2 * d2),
+                (base - apart, n2 * d1 - n1 * d2),
             )):
                 turn_c, turn_s = turns[at]
                 row_c, row_s = rows_ref[rows, 2 + 2 * at : 3 + 2 * at], rows_ref[rows, 3 + 2 * at : 4 + 2 * at]
@@ -277,7 +278,7 @@
                 put(6 * at + 4, even_r - odd_i)
                 put(6 * at + 5, even_i + odd_r)
 
-        return [functools.partial(step, part) for part in range(SIDE // 16)]
+        return [functools.partial(step, part) for part in range(CELLS)]
 
     def transform(slot, waiting):
         def mix_some(count):
@@ -299,7 +300,7 @@
                 k = 768 * at + 256 * rest
                 r = dot(left_refs[slot % 2][:, k : k + 256], first_ref[k : k + 256, :])
                 put_rows(r, columns[column_class(at + 1, rest)])
-                mix_some(1)
+                mix_some(2)
         put_rows(dot(left_refs[slot % 2][:, 1536:1792], first_ref[1536:1792, :]), 768)
         mix_some(1)
         put_rows(dot(left_refs[slot % 2][:, 1792:1920], first_ref[1792:1920, :]), 896)
@@ -326,7 +327,7 @@
                         total = -total if half > odd else total
                         base = SIDE * odd + HALF * half
                         s_ref[base : base + HALF, :] = total.astype(bf16)
-                mix_some(2)
+                mix_some(1 if n % 2 else 0)
 
         even_part = dot(fwd_ref[0:SIDE, :], s_ref[0:SIDE, :])
         odd_part = lax.dot_general(

time: 63.4 us -> 61.7 us (0.973)
  Pallas kernels: 18.7 us -> 17 us
    pallas_call x1, Pallas kernels: 16.9 us -> 15.2 us  [tile_results(): pl.pallas_call(functools.partial(tile_kernel, devices, group_count), out_...]
where the time goes in v5:
time: 61.7 us; the launch traced here: 61.4 us
  blocking collectives  35.6 us (58%)
  Pallas kernels  17 us (28%)
  starting transfers between devices  5.04 us (8%)
  waiting for transfers between devices  3.78 us (6%)
    all_to_all x1, blocking collectives, shards(): spread = lax.all_to_all(results, 'ty', 0, 0, tiled=True)  22.2 us
    pallas_call x1, Pallas kernels, tile_results(): pl.pallas_call(functools.partial(tile_kernel, devices, group_count), out_...  15.2 us
    all_to_all x1, blocking collectives, shards(): home = lax.all_to_all(picked(spread, slots), 'ty', 0, 0, tiled=True)  13.3 us
    ppermute x1, starting transfers between devices, shards(): lax.ppermute(home[:, :ROW_GROUPS], 'tx', [(g, g - 1) for g in range(1, gr...  5.04 us
    ppermute x1, waiting for transfers between devices, shards(): lax.ppermute(home[:, :ROW_GROUPS], 'tx', [(g, g - 1) for g in range(1, gr...  3.78 us
  transfers between devices with their start and end apart: 1, of which 1 were waited for; matrix products, arithmetic and copies ran while one was open for 0% of the time, Pallas kernels for 0%

profile of v5, /device:TPU:1, one launch (start us, length us, event | category | flops | bytes accessed | tf_op | source)
XLA Modules:
  0.0 61.4 jit_solution(9013991379015416426)
XLA Ops:
  0.0 15.2 %tiles.1 = bf16[16,28,8,128]{3,2,1,0:T(8,128)(2,1)} custom-call(s32[1,3]{1,0:T(1,128)} %names_ref.1, f32[1,3]{1,0:T(1,128)} %bitcast.9, bf16[3,5,384,384]{3,2,1,0:T(8,128)(2,1)} %bitcast.7, s32[3,12,1,12]{3,2,1,0:T(1,128)} %bitcast.8, f32[384,384]{1,0:T(8,128)} %otf_hbm.1, f32[384,384]{1,0:T(8,128)} %apod_hbm.1, f32[384,6]{1,0:T(8,128)} %constant.10.clone.rows_hbm, ...), custom_call_target="tpu_custom_call" | custom-call | flops 6000000000 | bytes 10000000 | tf_op jit(solution)/shard_map/tiles/pallas_call | solution.py:426
  15.2 22.2 %all_to_all.10 = bf16[16,28,8,128]{3,2,1,0:T(8,128)(2,1)S(1)} all-to-all(bf16[16,28,8,128]{3,2,1,0:T(8,128)(2,1)} %tiles.1), channel_id=1, replica_groups=mesh['tx'=8,'ty'=16] {'ty'}, dimensions={0} | all-to-all | bytes 1835008 | tf_op jit(solution)/shard_map/all_to_all | solution.py:528
  37.4 0.8 %pick.1 = bf16[288,8,128]{2,1,0:T(8,128)(2,1)S(1)} custom-call(bf16[448,8,128]{2,1,0:T(8,128)(2,1)S(1)} %bitcast.5), custom_call_target="tpu_custom_call" | custom-call | tf_op jit(solution)/shard_map/pick/pallas_call | solution.py:483
  38.2 13.3 %all_to_all.11.in_ref = bf16[16,18,8,128]{3,2,1,0:T(8,128)(2,1)S(1)} all-to-all(bf16[16,18,8,128]{3,2,1,0:T(8,128)(2,1)S(1)} %bitcast.6), channel_id=1, replica_groups=mesh['tx'=8,'ty'=16] {'ty'}, dimensions={0} | all-to-all | bytes 1179648 | tf_op jit(solution)/shard_map/all_to_all | solution.py:529
  51.5 5.0 %collective-permute-start = (bf16[16,3,8,128]{3,2,1,0:T(8,128)(2,1)S(1)}, bf16[16,3,8,128]{3,2,1,0:T(8,128)(2,1)S(1)}, u32[]{:S(2)}, u32[]{:S(2)}) collective-permute-start(bf16[16,3,8,128]{3,2,1,0:T(8,128)(2,1)S(1)} %slice.4), channel_id=1, source_target_pairs={{16,0},{32,16},{48,32},{64,48},{80,64},{96,80},{112,96},{17,1},{33... | collective-permute-start | bytes 294920 | tf_op jit(solution)/shard_map/ppermute | solution.py:530
  56.6 3.8 %collective-permute-done.strip_ref = bf16[16,3,8,128]{3,2,1,0:T(8,128)(2,1)S(1)} collective-permute-done((bf16[16,3,8,128]{3,2,1,0:T(8,128)(2,1)S(1)}, bf16[16,3,8,128]{3,2,1,0:T(8,128)(2,1)S(1)}, u32[]{:S(2)}, u32[]{:S(2)}) %collective-permute-start) | collective-permute-done | bytes 98336 | tf_op jit(solution)/shard_map/ppermute | solution.py:530
  60.4 1.1 %join.1 = f32[320,640]{1,0:T(8,128)} custom-call(bf16[16,18,8,128]{3,2,1,0:T(8,128)(2,1)S(1)} %all_to_all.11.in_ref, bf16[16,3,8,128]{3,2,1,0:T(8,128)(2,1)S(1)} %collective-permute-done.strip_ref), custom_call_target="tpu_custom_call" | custom-call | tf_op jit(solution)/shard_map/join/pallas_call | solution.py:532
  (1 shorter events, 0.0 us)
Async XLA Ops:
  51.5 8.8 %collective-permute-start = (bf16[16,3,8,128]{3,2,1,0:T(8,128)(2,1)S(1)}, bf16[16,3,8,128]{3,2,1,0:T(8,128)(2,1)S(1)}, u32[]{:S(2)}, u32[]{:S(2)}) collective-permute-start(bf16[16,3,8,128]{3,2,1,0:T(8,128)(2,1)S(1)} %slice.4), channel_id=1, source_target_pairs={{16,0},{32,16},{48,32},{64,48},{80,64},{96,80},{112,96},{17,1},{33... | collective-permute-start | bytes 294920 | tf_op jit(solution)/shard_map/ppermute | solution.py:530

commit v6 on v5

--- a/solution.py
+++ b/solution.py
@@ -506,16 +506,30 @@
     return jnp.concatenate(body, axis=0)
 
 
-def join_kernel(in_ref, strip_ref, out_ref):
+def join_kernel(in_ref, out_ref):
     low = lax.broadcasted_iota(jnp.int32, (STRIDE, 128), 1) < OVERLAP
     left = [pltpu.roll(folded(in_ref, ROW_GROUPS * tile), OVERLAP, 1) for tile in range(3)]
-    right = [folded(in_ref, TILE_GROUPS + ROW_GROUPS * tile) for tile in range(3)]
+    right = [folded(in_ref, TILE_GROUPS + ROW_GROUPS * tile) for tile in range(2)]
     out_ref[:, 0:128] = jnp.where(low, left[0], left[1])
     out_ref[:, 128:256] = jnp.where(low, left[1], left[2])
     out_ref[:, 256:384] = right[0] + jnp.where(low, left[2], 0.0)
     out_ref[:, 384:512] = right[1]
+
+
+def join_main_kernel(in_ref, out_ref, body_ref, sem):
+    join_kernel(in_ref, body_ref)
+    copy = pltpu.make_async_copy(body_ref, out_ref.at[:, 0:512], sem)
+    copy.start()
+    copy.wait()
+
+
+def edge_kernel(in_ref, strip_ref, joined_ref, out_ref, edge_ref, sem):
+    low = lax.broadcasted_iota(jnp.int32, (STRIDE, 128), 1) < OVERLAP
     strip = pltpu.roll(folded(strip_ref, 0), OVERLAP, 1)
-    out_ref[:, 512:640] = right[2] + jnp.where(low, 0.0, strip)
+    edge_ref[...] = folded(in_ref, TILE_GROUPS + 2 * ROW_GROUPS) + jnp.where(low, 0.0, strip)
+    copy = pltpu.make_async_copy(edge_ref, out_ref.at[:, 512:640], sem)
+    copy.start()
+    copy.wait()
 
 
 def shards(frames, masks, phases, slot_tile, otf, apod):
@@ -529,13 +543,20 @@
     home = lax.all_to_all(picked(spread, slots), "ty", 0, 0, tiled=True)
     strip = lax.ppermute(home[:, :ROW_GROUPS], "tx", [(g, g - 1) for g in range(1, group_count)])
     in_vmem = pl.BlockSpec(memory_space=pltpu.VMEM)
+    place = jax.ShapeDtypeStruct((STRIDE, STRIDE * GROUP_COLS), jnp.float32)
+    anywhere = pl.BlockSpec(memory_space=pl.ANY)
+    small = pltpu.CompilerParams(vmem_limit_bytes=SMALL_VMEM)
+    joined = pl.pallas_call(
+        join_main_kernel, out_shape=place, in_specs=[in_vmem], out_specs=anywhere,
+        scratch_shapes=[pltpu.VMEM((STRIDE, 512), jnp.float32), pltpu.SemaphoreType.DMA],
+        cost_estimate=pl.CostEstimate(flops=2_000_000_000, bytes_accessed=1_400_000, transcendentals=0),
+        compiler_params=small, name="join",
+    )(home)
     return pl.pallas_call(
-        join_kernel,
-        out_shape=jax.ShapeDtypeStruct((STRIDE, STRIDE * GROUP_COLS), jnp.float32),
-        in_specs=[in_vmem, in_vmem], out_specs=in_vmem,
-        compiler_params=pltpu.CompilerParams(vmem_limit_bytes=SMALL_VMEM),
-        name="join",
-    )(home, strip)
+        edge_kernel, out_shape=place, in_specs=[in_vmem, in_vmem, anywhere], out_specs=anywhere,
+        scratch_shapes=[pltpu.VMEM((STRIDE, 128), jnp.float32), pltpu.SemaphoreType.DMA],
+        input_output_aliases={2: 0}, compiler_params=small, name="edge",
+    )(home, strip, joined)
 
 
 def solution(mesh):

time: 61.7 us -> 61.4 us (level)
  waiting for transfers between devices: 3.78 us -> 2.77 us
  Pallas kernels: 17 us -> 17.7 us
    ppermute x1, waiting for transfers between devices: 3.78 us -> 2.77 us  [shards(): lax.ppermute(home[:, :ROW_GROUPS], 'tx', [(g, g - 1) for g in range(1, gr...]
    pallas_call x1 -> x2, Pallas kernels: 1.07 us -> 1.77 us  [the longest x1 1 us: shards(): pl.pallas_call(join_main_kernel, out_shape=place, in_specs=[in_vmem], out...]
  transfers between devices with their start and end apart: 1 -> 1, of which waited for: 1 -> 1; matrix products, arithmetic and copies ran while one was open for 0% -> 0% of each run, Pallas kernels for 0% -> 2%
where the time goes in v6:
time: 61.4 us; the launch traced here: 61.1 us
  blocking collectives  35.6 us (58%)
  Pallas kernels  17.7 us (29%)
  starting transfers between devices  5.04 us (8%)
  waiting for transfers between devices  2.77 us (5%)
    all_to_all x1, blocking collectives, shards(): spread = lax.all_to_all(results, 'ty', 0, 0, tiled=True)  22.2 us
    pallas_call x1, Pallas kernels, tile_results(): pl.pallas_call(functools.partial(tile_kernel, devices, group_count), out_...  15.2 us
    all_to_all x1, blocking collectives, shards(): home = lax.all_to_all(picked(spread, slots), 'ty', 0, 0, tiled=True)  13.3 us
    ppermute x1, starting transfers between devices, shards(): lax.ppermute(home[:, :ROW_GROUPS], 'tx', [(g, g - 1) for g in range(1, gr...  5.04 us
    ppermute x1, waiting for transfers between devices, shards(): lax.ppermute(home[:, :ROW_GROUPS], 'tx', [(g, g - 1) for g in range(1, gr...  2.77 us
  transfers between devices with their start and end apart: 1, of which 1 were waited for; matrix products, arithmetic and copies ran while one was open for 0% of the time, Pallas kernels for 2%

profile of v6, /device:TPU:1, one launch (start us, length us, event | category | flops | bytes accessed | tf_op | source)
XLA Modules:
  0.0 61.1 jit_solution(10608478360816704397)
XLA Ops:
  0.0 15.2 %tiles.1 = bf16[16,28,8,128]{3,2,1,0:T(8,128)(2,1)} custom-call(s32[1,3]{1,0:T(1,128)} %names_ref.1, f32[1,3]{1,0:T(1,128)} %bitcast.9, bf16[3,5,384,384]{3,2,1,0:T(8,128)(2,1)} %bitcast.7, s32[3,12,1,12]{3,2,1,0:T(1,128)} %bitcast.8, f32[384,384]{1,0:T(8,128)} %otf_hbm.1, f32[384,384]{1,0:T(8,128)} %apod_hbm.1, f32[384,6]{1,0:T(8,128)} %constant.10.clone.rows_hbm, ...), custom_call_target="tpu_custom_call" | custom-call | flops 6000000000 | bytes 10000000 | tf_op jit(solution)/shard_map/tiles/pallas_call | solution.py:426
  15.2 22.2 %all_to_all.10 = bf16[16,28,8,128]{3,2,1,0:T(8,128)(2,1)S(1)} all-to-all(bf16[16,28,8,128]{3,2,1,0:T(8,128)(2,1)} %tiles.1), channel_id=1, replica_groups=mesh['tx'=8,'ty'=16] {'ty'}, dimensions={0} | all-to-all | bytes 1835008 | tf_op jit(solution)/shard_map/all_to_all | solution.py:542
  37.4 0.8 %pick.1 = bf16[288,8,128]{2,1,0:T(8,128)(2,1)S(1)} custom-call(bf16[448,8,128]{2,1,0:T(8,128)(2,1)S(1)} %bitcast.5), custom_call_target="tpu_custom_call" | custom-call | tf_op jit(solution)/shard_map/pick/pallas_call | solution.py:483
  38.2 13.3 %all_to_all.11.in_ref = bf16[16,18,8,128]{3,2,1,0:T(8,128)(2,1)S(1)} all-to-all(bf16[16,18,8,128]{3,2,1,0:T(8,128)(2,1)S(1)} %bitcast.6), channel_id=1, replica_groups=mesh['tx'=8,'ty'=16] {'ty'}, dimensions={0} | all-to-all | bytes 1179648 | tf_op jit(solution)/shard_map/all_to_all | solution.py:543
  51.5 5.0 %collective-permute-start = (bf16[16,3,8,128]{3,2,1,0:T(8,128)(2,1)S(1)}, bf16[16,3,8,128]{3,2,1,0:T(8,128)(2,1)S(1)}, u32[]{:S(2)}, u32[]{:S(2)}) collective-permute-start(bf16[16,3,8,128]{3,2,1,0:T(8,128)(2,1)S(1)} %slice.4), channel_id=1, source_target_pairs={{16,0},{32,16},{48,32},{64,48},{80,64},{96,80},{112,96},{17,1},{33... | collective-permute-start | bytes 294920 | tf_op jit(solution)/shard_map/ppermute | solution.py:544
  56.6 1.0 %join.1.joined_ref = f32[320,640]{1,0:T(8,128)} custom-call(bf16[16,18,8,128]{3,2,1,0:T(8,128)(2,1)S(1)} %all_to_all.11.in_ref), custom_call_target="tpu_custom_call" | custom-call | flops 2000000000 | bytes 1400000 | tf_op jit(solution)/shard_map/join/pallas_call | solution.py:549
  57.6 2.8 %collective-permute-done.strip_ref = bf16[16,3,8,128]{3,2,1,0:T(8,128)(2,1)S(1)} collective-permute-done((bf16[16,3,8,128]{3,2,1,0:T(8,128)(2,1)S(1)}, bf16[16,3,8,128]{3,2,1,0:T(8,128)(2,1)S(1)}, u32[]{:S(2)}, u32[]{:S(2)}) %collective-permute-start) | collective-permute-done | bytes 98336 | tf_op jit(solution)/shard_map/ppermute | solution.py:544
  60.4 0.8 %edge.1 = f32[320,640]{1,0:T(8,128)} custom-call(bf16[16,18,8,128]{3,2,1,0:T(8,128)(2,1)S(1)} %all_to_all.11.in_ref, bf16[16,3,8,128]{3,2,1,0:T(8,128)(2,1)S(1)} %collective-permute-done.strip_ref, f32[320,640]{1,0:T(8,128)} %join.1.joined_ref), custom_call_target="tpu_custom_call", output_to_operand_aliasing={{}: (2, {})} | custom-call | tf_op jit(solution)/shard_map/edge/pallas_call | solution.py:555
  (1 shorter events, 0.0 us)
Async XLA Ops:
  51.5 8.8 %collective-permute-start = (bf16[16,3,8,128]{3,2,1,0:T(8,128)(2,1)S(1)}, bf16[16,3,8,128]{3,2,1,0:T(8,128)(2,1)S(1)}, u32[]{:S(2)}, u32[]{:S(2)}) collective-permute-start(bf16[16,3,8,128]{3,2,1,0:T(8,128)(2,1)S(1)} %slice.4), channel_id=1, source_target_pairs={{16,0},{32,16},{48,32},{64,48},{80,64},{96,80},{112,96},{17,1},{33... | collective-permute-start | bytes 294920 | tf_op jit(solution)/shard_map/ppermute | solution.py:544

commit v7 on v6

--- a/solution.py
+++ b/solution.py
@@ -247,8 +247,8 @@
             return a + both, a - 0.5 * both, (0.5 * math.sqrt(3.0)) * (b - c)
 
         def step(part):
-            rows = pl.ds(32 * part, 32)
-            flag = jnp.broadcast_to(flags[part : part + 1, :], (32, SIDE)).astype(bf16)
+            rows = pl.ds(64 * part, 64)
+            flag = jnp.concatenate([jnp.broadcast_to(flags[2 * part + at : 2 * part + at + 1, :], (32, SIDE)) for at in range(2)], axis=0).astype(bf16)
             f = [(frames_ref[now, p, rows, :] * flag).astype(f32) for p in range(PHASES)]
             a1, d1, a2, d2 = f[1] + f[4], f[1] - f[4], f[2] + f[3], f[2] - f[3]
 
@@ -278,7 +278,7 @@
                 put(6 * at + 4, even_r - odd_i)
                 put(6 * at + 5, even_i + odd_r)
 
-        return [functools.partial(step, part) for part in range(CELLS)]
+        return [functools.partial(step, part) for part in range(CELLS // 2)]
 
     def transform(slot, waiting):
         def mix_some(count):
@@ -300,7 +300,7 @@
                 k = 768 * at + 256 * rest
                 r = dot(left_refs[slot % 2][:, k : k + 256], first_ref[k : k + 256, :])
                 put_rows(r, columns[column_class(at + 1, rest)])
-                mix_some(2)
+                mix_some(1)
         put_rows(dot(left_refs[slot % 2][:, 1536:1792], first_ref[1536:1792, :]), 768)
         mix_some(1)
         put_rows(dot(left_refs[slot % 2][:, 1792:1920], first_ref[1792:1920, :]), 896)

time: 61.4 us -> 61.3 us (level)
  no operation moved by 1% of the time
where the time goes in v7:
time: 61.3 us; the launch traced here: 61 us
  blocking collectives  35.6 us (58%)
  Pallas kernels  17.6 us (29%)
  starting transfers between devices  5.04 us (8%)
  waiting for transfers between devices  2.8 us (5%)
    all_to_all x1, blocking collectives, shards(): spread = lax.all_to_all(results, 'ty', 0, 0, tiled=True)  22.2 us
    pallas_call x1, Pallas kernels, tile_results(): pl.pallas_call(functools.partial(tile_kernel, devices, group_count), out_...  15.1 us
    all_to_all x1, blocking collectives, shards(): home = lax.all_to_all(picked(spread, slots), 'ty', 0, 0, tiled=True)  13.3 us
    ppermute x1, starting transfers between devices, shards(): lax.ppermute(home[:, :ROW_GROUPS], 'tx', [(g, g - 1) for g in range(1, gr...  5.04 us
    ppermute x1, waiting for transfers between devices, shards(): lax.ppermute(home[:, :ROW_GROUPS], 'tx', [(g, g - 1) for g in range(1, gr...  2.8 us
  transfers between devices with their start and end apart: 1, of which 1 were waited for; matrix products, arithmetic and copies ran while one was open for 0% of the time, Pallas kernels for 2%

profile of v7, /device:TPU:1, one launch (start us, length us, event | category | flops | bytes accessed | tf_op | source)
XLA Modules:
  0.0 61.0 jit_solution(13809607476814032538)
XLA Ops:
  0.0 15.1 %tiles.1 = bf16[16,28,8,128]{3,2,1,0:T(8,128)(2,1)} custom-call(s32[1,3]{1,0:T(1,128)} %names_ref.1, f32[1,3]{1,0:T(1,128)} %bitcast.9, bf16[3,5,384,384]{3,2,1,0:T(8,128)(2,1)} %bitcast.7, s32[3,12,1,12]{3,2,1,0:T(1,128)} %bitcast.8, f32[384,384]{1,0:T(8,128)} %otf_hbm.1, f32[384,384]{1,0:T(8,128)} %apod_hbm.1, f32[384,6]{1,0:T(8,128)} %constant.10.clone.rows_hbm, ...), custom_call_target="tpu_custom_call" | custom-call | flops 6000000000 | bytes 10000000 | tf_op jit(solution)/shard_map/tiles/pallas_call | solution.py:426
  15.1 22.2 %all_to_all.10 = bf16[16,28,8,128]{3,2,1,0:T(8,128)(2,1)S(1)} all-to-all(bf16[16,28,8,128]{3,2,1,0:T(8,128)(2,1)} %tiles.1), channel_id=1, replica_groups=mesh['tx'=8,'ty'=16] {'ty'}, dimensions={0} | all-to-all | bytes 1835008 | tf_op jit(solution)/shard_map/all_to_all | solution.py:542
  37.3 0.8 %pick.1 = bf16[288,8,128]{2,1,0:T(8,128)(2,1)S(1)} custom-call(bf16[448,8,128]{2,1,0:T(8,128)(2,1)S(1)} %bitcast.5), custom_call_target="tpu_custom_call" | custom-call | tf_op jit(solution)/shard_map/pick/pallas_call | solution.py:483
  38.0 13.3 %all_to_all.11.in_ref = bf16[16,18,8,128]{3,2,1,0:T(8,128)(2,1)S(1)} all-to-all(bf16[16,18,8,128]{3,2,1,0:T(8,128)(2,1)S(1)} %bitcast.6), channel_id=1, replica_groups=mesh['tx'=8,'ty'=16] {'ty'}, dimensions={0} | all-to-all | bytes 1179648 | tf_op jit(solution)/shard_map/all_to_all | solution.py:543
  51.4 5.0 %collective-permute-start = (bf16[16,3,8,128]{3,2,1,0:T(8,128)(2,1)S(1)}, bf16[16,3,8,128]{3,2,1,0:T(8,128)(2,1)S(1)}, u32[]{:S(2)}, u32[]{:S(2)}) collective-permute-start(bf16[16,3,8,128]{3,2,1,0:T(8,128)(2,1)S(1)} %slice.4), channel_id=1, source_target_pairs={{16,0},{32,16},{48,32},{64,48},{80,64},{96,80},{112,96},{17,1},{33... | collective-permute-start | bytes 294920 | tf_op jit(solution)/shard_map/ppermute | solution.py:544
  56.4 1.0 %join.1.joined_ref = f32[320,640]{1,0:T(8,128)} custom-call(bf16[16,18,8,128]{3,2,1,0:T(8,128)(2,1)S(1)} %all_to_all.11.in_ref), custom_call_target="tpu_custom_call" | custom-call | flops 2000000000 | bytes 1400000 | tf_op jit(solution)/shard_map/join/pallas_call | solution.py:549
  57.5 2.8 %collective-permute-done.strip_ref = bf16[16,3,8,128]{3,2,1,0:T(8,128)(2,1)S(1)} collective-permute-done((bf16[16,3,8,128]{3,2,1,0:T(8,128)(2,1)S(1)}, bf16[16,3,8,128]{3,2,1,0:T(8,128)(2,1)S(1)}, u32[]{:S(2)}, u32[]{:S(2)}) %collective-permute-start) | collective-permute-done | bytes 98336 | tf_op jit(solution)/shard_map/ppermute | solution.py:544
  60.3 0.8 %edge.1 = f32[320,640]{1,0:T(8,128)} custom-call(bf16[16,18,8,128]{3,2,1,0:T(8,128)(2,1)S(1)} %all_to_all.11.in_ref, bf16[16,3,8,128]{3,2,1,0:T(8,128)(2,1)S(1)} %collective-permute-done.strip_ref, f32[320,640]{1,0:T(8,128)} %join.1.joined_ref), custom_call_target="tpu_custom_call", output_to_operand_aliasing={{}: (2, {})} | custom-call | tf_op jit(solution)/shard_map/edge/pallas_call | solution.py:555
  (1 shorter events, 0.0 us)
Async XLA Ops:
  51.4 8.9 %collective-permute-start = (bf16[16,3,8,128]{3,2,1,0:T(8,128)(2,1)S(1)}, bf16[16,3,8,128]{3,2,1,0:T(8,128)(2,1)S(1)}, u32[]{:S(2)}, u32[]{:S(2)}) collective-permute-start(bf16[16,3,8,128]{3,2,1,0:T(8,128)(2,1)S(1)} %slice.4), channel_id=1, source_target_pairs={{16,0},{32,16},{48,32},{64,48},{80,64},{96,80},{112,96},{17,1},{33... | collective-permute-start | bytes 294920 | tf_op jit(solution)/shard_map/ppermute | solution.py:544
